TPU v7x, 32 devices: a whole 2x2x4 slice. The times are simulated.
32 devices in a mesh: seq: 8 (over z, y), head: 4 (over x, core).
Axes of the slice: x: 2, y: 2, z: 4, core: 2. Of those that a mesh axis runs over, the one named last changes fastest.
Arguments:
- queries: bfloat16 [2048, 4096], P('seq', 'head'), may hold values from -80 to 80, as said below
- keys_in: bfloat16 [2048, 4096], P('seq', 'head'), may hold values from -4 to 4
- values_in: bfloat16 [2048, 4096], P('seq', 'head'), may hold values from -6 to 6
- out_weight: bfloat16 [4096, 4096], P('head'), may hold values from -0.09375 to 0.09375
- spans: int32 [32], P('head'), may hold values from 1024 to 4096
- full_ids: int32 [8], P('head'), may hold values from 0 to 31, as said below
Outputs:
- mixed: bfloat16 [2048, 4096], P('seq', 'head')
Inputs may be any that keep to these rules, and one draw needn't show every extreme that they name: `queries`: unlike a plain normal draw, some rows may be far larger than the rest. `full_ids`: increasing and distinct; entries g * 2 to (g + 1) * 2 - 1 name heads of group g, that is heads g * 8 to (g + 1) * 8 - 1.
All inputs are finite; a program needn't handle non-finite values.
Results may differ from a plain program's by a relative error of at most 0.012.
Values may be sent and summed in bfloat16 or wider, within the bound.
No kernel may reach another device: no remote copies, remote signals or barrier semaphores. Data moves between devices by JAX's collectives and lax.ppermute only.
A program may use at most 128 MiB of HBM per device.

v0:
```python
import math

import functools

import jax
import jax.numpy as jnp
from jax import lax
from jax.experimental import pallas as pl
from jax.experimental.pallas import tpu as pltpu
from jax.sharding import PartitionSpec as P

HEAD_DIM = 128
SPAN_MAX = 4096


NEG_FILL = -1e30


def from_behind(block, axis, distance):
    devices = range(lax.axis_size(axis))
    route = [(i - distance, i) for i in devices if i - distance in devices]
    return lax.ppermute(block, axis, route)


def online_update(carry_state, scores, allowed, value_rows):
    old_peak, row_total, numerator = carry_state
    masked = jnp.where(allowed, scores, NEG_FILL)
    new_peak = jnp.maximum(old_peak, jnp.max(masked, axis=-1))
    weights = jnp.where(allowed, jnp.exp(masked - new_peak[..., None]), 0.0)
    rescale = jnp.exp(old_peak - new_peak)
    row_total = row_total * rescale + jnp.sum(weights, axis=-1)
    numerator = numerator * rescale[..., None] + jnp.einsum(
        "hqk,hkd->hqd", weights.astype(jnp.bfloat16), value_rows, preferred_element_type=jnp.float32
    )
    return (new_peak, row_total, numerator)


def empty_state(lead_count, row_count, head_width):
    return (
        jnp.full((lead_count, row_count), NEG_FILL, jnp.float32),
        jnp.zeros((lead_count, row_count), jnp.float32),
        jnp.zeros((lead_count, row_count, head_width), jnp.float32),
    )


def finish(carry_state):
    return (carry_state[2] / carry_state[1][..., None]).astype(jnp.bfloat16)


def ring_path(queries, keys_in, values_in, out_weight, spans, full_ids):
    score_scale = HEAD_DIM ** (-0.5)
    n_seq = lax.axis_size("seq")
    seq_index = lax.axis_index("seq")
    tok_rows = queries.shape[0]
    group_heads = queries.shape[1] // HEAD_DIM
    full_count = full_ids.shape[0]
    band_count = group_heads - full_count
    head_base = lax.axis_index("head") * group_heads
    local_range = jnp.arange(group_heads)
    marks = jnp.sum(
        (local_range[:, None] + head_base == full_ids[None, :]).astype(jnp.int32), axis=1
    )
    order_local = jnp.argsort(marks * group_heads + local_range)
    band_local = order_local[:band_count]
    full_local = order_local[band_count:]
    query_three = queries.reshape(tok_rows, group_heads, HEAD_DIM)
    key_three = keys_in.reshape(tok_rows, group_heads, HEAD_DIM)
    value_three = values_in.reshape(tok_rows, group_heads, HEAD_DIM)
    query_band = jnp.take(query_three, band_local, axis=1).transpose(1, 0, 2)
    kv_band = jnp.stack(
        [
            jnp.take(key_three, band_local, axis=1).transpose(1, 0, 2),
            jnp.take(value_three, band_local, axis=1).transpose(1, 0, 2),
        ]
    )
    band_reach = jnp.take(spans, band_local)
    query_pos = seq_index * tok_rows + jnp.arange(tok_rows)
    hop_count = min(max(1, SPAN_MAX // tok_rows), n_seq - 1)
    arrived = [(kv_band, 0)]
    moving = kv_band
    for distance in range(1, hop_count + 1):
        moving = from_behind(moving, "seq", 1)
        arrived.append((moving, distance))
    batch_size = max(1, 512 // tok_rows)
    band_state = empty_state(band_count, tok_rows, HEAD_DIM)
    for first_piece in range(0, len(arrived), batch_size):
        batch_pieces = arrived[first_piece : first_piece + batch_size]
        key_rows = jnp.concatenate([arrival[0][0] for arrival in batch_pieces], axis=1)
        value_rows = jnp.concatenate([arrival[0][1] for arrival in batch_pieces], axis=1)
        key_pos = jnp.concatenate(
            [(seq_index - arrival[1]) * tok_rows + jnp.arange(tok_rows) for arrival in batch_pieces]
        )
        scores = (
            jnp.einsum("hqd,hkd->hqk", query_band, key_rows, preferred_element_type=jnp.float32)
            * score_scale
        )
        gap_size = query_pos[None, :, None] - key_pos[None, None, :]
        allowed = (
            (gap_size >= 0) & (gap_size < band_reach[:, None, None]) & (key_pos >= 0)[None, None, :]
        )
        band_state = online_update(band_state, scores, allowed, value_rows)
    band_out = finish(band_state)
    query_full = jnp.take(query_three, full_local, axis=1).transpose(1, 0, 2)
    key_full = jnp.take(key_three, full_local, axis=1).transpose(1, 0, 2)
    value_full = jnp.take(value_three, full_local, axis=1).transpose(1, 0, 2)
    kv_full = jnp.stack([key_full, value_full])
    last_query = seq_index * tok_rows + tok_rows - 1
    key_piece = lax.all_gather(kv_full, "seq", axis=2, tiled=True)
    row_count = key_piece.shape[2]
    tile_rows = math.gcd(row_count, 512)

    def absorb_tile(tile_index, inner_state):
        key_tile = lax.dynamic_slice_in_dim(key_piece[0], tile_index * tile_rows, tile_rows, 1)
        value_tile = lax.dynamic_slice_in_dim(key_piece[1], tile_index * tile_rows, tile_rows, 1)
        key_pos = tile_index * tile_rows + jnp.arange(tile_rows)
        scores = (
            jnp.einsum("hqd,hkd->hqk", query_full, key_tile, preferred_element_type=jnp.float32)
            * score_scale
        )
        allowed = key_pos[None, None, :] <= query_pos[None, :, None]
        return online_update(inner_state, scores, allowed, value_tile)

    live_tiles = jnp.clip(last_query // tile_rows + 1, 0, row_count // tile_rows)
    full_state = lax.fori_loop(
        0, live_tiles, absorb_tile, empty_state(full_count, tok_rows, HEAD_DIM)
    )
    full_out = finish(full_state)
    combined = jnp.concatenate([band_out, full_out], axis=0)
    inverse = jnp.argsort(order_local)
    per_head = jnp.take(combined, inverse, axis=0)
    attended = per_head.transpose(1, 0, 2).reshape(tok_rows, group_heads * HEAD_DIM)
    projected = jnp.dot(attended, out_weight, preferred_element_type=jnp.float32)
    return lax.psum_scatter(projected.astype(jnp.bfloat16), "head", scatter_dimension=1, tiled=True)


def move(block, axis, pairs):
    return lax.ppermute(block, axis, pairs)


def swap(block, axis, flip):
    return move(block, axis, [(i, i ^ flip) for i in range(lax.axis_size(axis))])


def in_vmem(count):
    return [pl.BlockSpec(memory_space=pltpu.VMEM)] * count


def held(array):
    return pltpu.with_memory_space_constraint(array, pltpu.VMEM)


SMEM = pl.BlockSpec(memory_space=pltpu.SMEM)
FACTOR = HEAD_DIM**-0.5 * math.log2(math.e)
STAT_ROWS = 16


def own_kernel(body, out_shapes, in_specs, scratch=(), flops=10**8, limit=20 * 2**20):
    return pl.pallas_call(
        body,
        out_shape=out_shapes,
        in_specs=in_specs,
        out_specs=in_vmem(len(out_shapes)),
        scratch_shapes=list(scratch),
        compiler_params=pltpu.CompilerParams(vmem_limit_bytes=limit),
        cost_estimate=pl.CostEstimate(flops=flops, bytes_accessed=10**6, transcendentals=0),
    )


def deal(half, me_ref, q_ref, k_ref, v_ref, *refs):
    inner, cross, cross_v = refs[:half], refs[half : 2 * half], refs[2 * half : 3 * half]
    sems = refs[3 * half]
    me = me_ref[0]
    low = me % half
    rows = q_ref.shape[0]
    waits = []

    def fetch(source, head, out_ref, place):
        at = pl.multiple_of(head * HEAD_DIM, HEAD_DIM)
        return pltpu.make_async_copy(
            source.at[:, pl.ds(at, HEAD_DIM)],
            out_ref.at[pl.ds(place * rows, rows)],
            sems.at[len(waits)],
        )

    for flip in range(half - 1, -1, -1):
        target = low ^ flip
        for place in range(6):
            source = (q_ref, k_ref, v_ref)[place % 3]
            copy = fetch(source, target + place // 3 * half, inner[flip], place)
            copy.start()
            waits.append(copy)
    for flip in range(half - 1, -1, -1):
        target = low ^ flip
        below = fetch(k_ref, target + half, cross[flip], 0)
        above = fetch(q_ref, target, cross[flip], 0)
        pl.when(me < half)(below.start)
        pl.when(me >= half)(above.start)
        waits.append(above)
        copy = fetch(v_ref, target + half, cross_v[flip], 0)
        copy.start()
        waits.append(copy)
    for copy in waits:
        copy.wait()


def square_eye(size):
    row = lax.broadcasted_iota(jnp.int32, (size, size), 0)
    return row == lax.broadcasted_iota(jnp.int32, (size, size), 1)


def pack_stat(stat):
    eye = square_eye(HEAD_DIM)
    rows = []
    for first in range(0, stat.shape[0], HEAD_DIM):
        piece = jnp.where(eye, stat[first : first + HEAD_DIM], 0.0)
        left = jnp.sum(piece, axis=0, keepdims=True)
        for _ in range(3):
            part = left.astype(jnp.bfloat16).astype(jnp.float32)
            rows.append(part)
            left = left - part
    rows.append(jnp.zeros((STAT_ROWS - len(rows), HEAD_DIM), jnp.float32))
    return jnp.concatenate(rows, axis=0).astype(jnp.bfloat16)


def unpack_stat(packed, size):
    eye = square_eye(HEAD_DIM)
    columns = []
    packed = packed.astype(jnp.float32)
    for index in range(size // HEAD_DIM):
        row = packed[3 * index : 3 * index + 1]
        for more in (1, 2):
            row = row + packed[3 * index + more : 3 * index + more + 1]
        columns.append(jnp.sum(jnp.where(eye, row, 0.0), axis=1, keepdims=True))
    return jnp.concatenate(columns, axis=0)


def softmax_rows(pieces, value_tiles):
    peak = jnp.max(functools.reduce(jnp.maximum, pieces), axis=1, keepdims=True)
    total, numerator = None, None
    for scores, value_tile in zip(pieces, value_tiles):
        weights = jnp.exp2((scores - peak) * FACTOR)
        total = weights if total is None else total + weights
        product = jnp.dot(
            weights.astype(jnp.bfloat16), value_tile, preferred_element_type=jnp.float32
        )
        numerator = product if numerator is None else numerator + product
    return numerator, jnp.sum(total, axis=1, keepdims=True), peak


def score_tile(q_tile, k_tile):
    return lax.dot_general(
        q_tile, k_tile, (((1,), (1,)), ((), ())), preferred_element_type=jnp.float32
    )


def attend_own_half(half, me_ref, *refs):
    inner, out_refs = refs[:half], refs[half : 2 * half]
    num_ref, total_ref, peak_ref, qkv, o_low, o_up, stats = refs[2 * half :]
    low = me_ref[0] % half
    block = out_refs[0].shape[0] // 2
    for flip in range(half):
        at = pl.multiple_of((low ^ flip) * block, block)
        for place in range(6):
            qkv[place, pl.ds(at, block)] = inner[flip][place * block : (place + 1) * block]
    row = lax.broadcasted_iota(jnp.int32, (block, block), 0)
    causal = row >= lax.broadcasted_iota(jnp.int32, (block, block), 1)
    for head in range(2):
        for i in range(half):
            q_tile = qkv[3 * head, i * block : (i + 1) * block]
            pieces, value_tiles = [], []
            for j in range(i + 1):
                scores = score_tile(q_tile, qkv[3 * head + 1, j * block : (j + 1) * block])
                pieces.append(jnp.where(causal, scores, NEG_FILL) if i == j else scores)
                value_tiles.append(qkv[3 * head + 2, j * block : (j + 1) * block])
            numerator, total, peak = softmax_rows(pieces, value_tiles)
            result = (numerator / total).astype(jnp.bfloat16)
            if head == 0:
                o_low[i] = result
                stats[i] = pack_stat(peak * FACTOR + jnp.log2(total))
            else:
                o_up[i] = result
                num_ref[i] = numerator
                total_ref[i] = total
                peak_ref[i] = peak
    for flip in range(half):
        out_refs[flip][:block] = o_low[low ^ flip]

        @pl.when(me_ref[0] < half)
        def _():
            out_refs[flip][block:] = o_up[low ^ flip]

        @pl.when(me_ref[0] >= half)
        def _():
            out_refs[flip][block : block + STAT_ROWS] = stats[low ^ flip]


def weigh_across(half, me_ref, spans_ref, full_ref, *refs):
    inner, cross = refs[:half], refs[half : 2 * half]
    weight_ref, total_ref, peak_ref, q_tiles, k_tiles = refs[2 * half :]
    me, head = me_ref[0], me_ref[1]
    low = me % half
    block = q_tiles.shape[1]
    below = me < half

    @pl.when(below)
    def _():
        for other in range(half):
            q_tiles[other] = cross[other][...]
            k_tiles[other] = inner[other][block : 2 * block]

    @pl.when(jnp.logical_not(below))
    def _():
        for other in range(half):
            q_tiles[other] = inner[other][3 * block : 4 * block]
            k_tiles[other] = cross[other][...]

    local = jnp.where(below, low, low + half)
    reach = spans_ref[local]
    for place in range(full_ref.shape[0]):
        reach = jnp.where(full_ref[place] == head * 2 * half + local, 2 * half * block, reach)
    row = lax.broadcasted_iota(jnp.int32, (block, block), 0)
    gap = row - lax.broadcasted_iota(jnp.int32, (block, block), 1)
    for flip in range(half):
        pieces = []
        for other in range(half):
            offset = (half + (low ^ flip) - (low ^ other)) * block
            scores = score_tile(q_tiles[flip], k_tiles[other])
            pieces.append(jnp.where(gap < reach - offset, scores, NEG_FILL))
        peak = jnp.max(functools.reduce(jnp.maximum, pieces), axis=1, keepdims=True)
        total = None
        for other in range(half):
            weights = jnp.exp2((pieces[other] - peak) * FACTOR)
            weight_ref[flip, :, other * block : (other + 1) * block] = weights.astype(jnp.bfloat16)
            total = weights if total is None else total + weights
        total_ref[flip] = jnp.sum(total, axis=1, keepdims=True)
        peak_ref[flip] = peak


def attend_across(half, flip, me_ref, num_ref, total_ref, peak_ref, *refs):
    weight_ref, far_total_ref, far_peak_ref = refs[:3]
    inner, cross_v = refs[3 : 3 + half], refs[3 + half : 3 + 2 * half]
    out_ref, values = refs[3 + 2 * half :]
    me = me_ref[0]
    block = out_ref.shape[0] - STAT_ROWS
    below = me < half

    @pl.when(below)
    def _():
        for other in range(half):
            values[other * block : (other + 1) * block] = inner[other][2 * block : 3 * block]

    @pl.when(jnp.logical_not(below))
    def _():
        for other in range(half):
            values[other * block : (other + 1) * block] = cross_v[other][...]

    numerator = jnp.dot(weight_ref[flip], values[...], preferred_element_type=jnp.float32)
    row_block = me % half ^ flip
    total, peak = far_total_ref[flip], far_peak_ref[flip]
    own_peak = jnp.where(below, NEG_FILL, peak_ref[row_block])
    joint = jnp.maximum(peak, own_peak)
    scale = jnp.exp2((peak - joint) * FACTOR)
    own_scale = jnp.where(below, 0.0, jnp.exp2((own_peak - joint) * FACTOR))
    numerator = numerator * scale + num_ref[row_block] * own_scale
    total = total * scale + total_ref[row_block] * own_scale
    out_ref[:block] = (numerator / total).astype(jnp.bfloat16)
    out_ref[block:] = pack_stat(joint * FACTOR + jnp.log2(total))


def join_heads(half, me_ref, *refs):
    own, across, upper = refs[:half], refs[half : 2 * half], refs[2 * half : 3 * half]
    joined = refs[3 * half]
    me = me_ref[0]
    low = me % half
    block = joined.shape[0]
    for flip in range(half):
        at = pl.multiple_of((low ^ flip) * HEAD_DIM, HEAD_DIM)
        up_at = pl.multiple_of((low ^ flip) * HEAD_DIM + half * HEAD_DIM, HEAD_DIM)

        @pl.when(me < half)
        def _():
            joined[:, pl.ds(at, HEAD_DIM)] = own[flip][:block]
            joined[:, pl.ds(up_at, HEAD_DIM)] = own[flip][block:]

        @pl.when(me >= half)
        def _():
            here = unpack_stat(own[flip][block : block + STAT_ROWS], block)
            there = unpack_stat(across[flip][block:], block)
            joint = jnp.maximum(here, there)
            here, there = jnp.exp2(here - joint), jnp.exp2(there - joint)
            total = here + there
            mixed = own[flip][:block].astype(jnp.float32) * (here / total)
            mixed = mixed + across[flip][:block].astype(jnp.float32) * (there / total)
            joined[:, pl.ds(at, HEAD_DIM)] = mixed.astype(jnp.bfloat16)
            joined[:, pl.ds(up_at, HEAD_DIM)] = upper[flip][:block]


def project(flip, part, parts, me_ref, joined, w_ref, out_ref):
    width = out_ref.shape[1]
    at = pl.multiple_of(((me_ref[1] ^ flip) * parts + part) * width, width)
    out_ref[...] = jnp.dot(
        joined[...], w_ref[:, pl.ds(at, width)], preferred_element_type=jnp.float32
    ).astype(jnp.bfloat16)


def half_path(queries, keys_in, values_in, out_weight, spans, full_ids):
    n_seq = lax.axis_size("seq")
    half = n_seq // 2
    bf16, f32 = jnp.bfloat16, jnp.float32
    shape = jax.ShapeDtypeStruct
    where = jnp.stack([lax.axis_index("seq"), lax.axis_index("head")]).astype(jnp.int32)
    block = queries.shape[0]
    down = range(half - 1, -1, -1)
    piece = shape((block, HEAD_DIM), bf16)

    dealt = own_kernel(
        functools.partial(deal, half),
        [shape((6 * block, HEAD_DIM), bf16)] * half + [piece] * (2 * half),
        [SMEM] + [pl.BlockSpec(memory_space=pltpu.HBM)] * 3,
        [pltpu.SemaphoreType.DMA((8 * half,))],
    )(where, *[pltpu.with_memory_space_constraint(a, pltpu.HBM) for a in (queries, keys_in, values_in)])
    inner, cross, cross_v = dealt[:half], dealt[half : 2 * half], dealt[2 * half :]
    inner, cross, cross_v = list(inner), list(cross), list(cross_v)
    for flip in range(half - 1, 0, -1):
        inner[flip] = swap(inner[flip], "seq", flip)
    for flip in down:
        cross[flip] = swap(cross[flip], "seq", half + flip)
    for flip in down:
        cross_v[flip] = move(cross_v[flip], "seq", [(i, half + (i ^ flip)) for i in range(half)])
    w_held = held(out_weight)
    inner = [held(a) for a in inner]
    cross = [held(a) for a in cross]
    cross_v = [held(a) for a in cross_v]

    *own, numerator, total, peak = own_kernel(
        functools.partial(attend_own_half, half),
        [shape((2 * block, HEAD_DIM), bf16)] * half
        + [shape((half, block, HEAD_DIM), f32)]
        + [shape((half, block, 1), f32)] * 2,
        [SMEM] + in_vmem(half),
        [
            pltpu.VMEM((6, half * block, HEAD_DIM), bf16),
            pltpu.VMEM((half, block, HEAD_DIM), bf16),
            pltpu.VMEM((half, block, HEAD_DIM), bf16),
            pltpu.VMEM((half, STAT_ROWS, HEAD_DIM), bf16),
        ],
        flops=2 * 10**9,
    )(where, *inner)
    for flip in range(half - 1, 0, -1):
        own[flip] = swap(own[flip], "seq", flip)
    weights = own_kernel(
        functools.partial(weigh_across, half),
        [shape((half, block, half * block), bf16)] + [shape((half, block, 1), f32)] * 2,
        [SMEM] * 3 + in_vmem(2 * half),
        [pltpu.VMEM((half, block, HEAD_DIM), bf16)] * 2,
        flops=2 * 10**9,
    )(where, spans, full_ids, *inner, *cross)
    state = [held(a) for a in (numerator, total, peak, *weights)]
    across, upper = [None] * half, [None] * half
    for flip in down:
        (sent,) = own_kernel(
            functools.partial(attend_across, half, flip),
            [shape((block + STAT_ROWS, HEAD_DIM), bf16)],
            [SMEM] + in_vmem(6 + 2 * half),
            [pltpu.VMEM((half * block, HEAD_DIM), bf16)],
            flops=5 * 10**8,
        )(where, *state, *inner, *cross_v)
        across[flip] = move(sent, "seq", [(i, half + (i ^ flip)) for i in range(half)])
        upper[flip] = sent
        if flip:
            upper[flip] = move(sent, "seq", [(half + i, half + (i ^ flip)) for i in range(half)])
    (joined,) = own_kernel(
        functools.partial(join_heads, half),
        [shape((block, n_seq * HEAD_DIM), bf16)],
        [SMEM] + in_vmem(3 * half),
    )(where, *[held(a) for a in own + across + upper])
    joined = held(joined)

    width = out_weight.shape[1] // lax.axis_size("head")

    def columns_of(flip, part, parts, rows):
        return own_kernel(
            functools.partial(project, flip, part, parts),
            [shape((block, width // parts), bf16)],
            [SMEM] + in_vmem(2),
            flops=10**9 // parts,
        )(where, rows, w_held)[0]

    def summed(came, kept):
        return (came.astype(f32) + kept.astype(f32)).astype(bf16)

    parts = 2
    sent = [columns_of(3, part, parts, joined) for part in range(parts)]
    came = [swap(a, "head", 1) for a in sent]
    rows, _ = lax.optimization_barrier((joined, sent[-1]))
    kept = [columns_of(2, part, parts, held(rows)) for part in range(parts)]
    far = [summed(a, b) for a, b in zip(came, kept)]
    rows, *far = lax.optimization_barrier((joined, *far))
    far = [swap(a, "head", 2) for a in far]
    near = columns_of(1, 0, 1, held(rows))
    near = swap(near, "head", 1)
    near = summed(near, columns_of(0, 0, 1, held(rows)))
    return (near.astype(f32) + jnp.concatenate(far, axis=1).astype(f32)).astype(bf16)


def on_device(queries, keys_in, values_in, out_weight, spans, full_ids):
    n_seq, n_head = lax.axis_size("seq"), lax.axis_size("head")
    block = queries.shape[0]
    one_head_each = queries.shape[1] == n_seq * HEAD_DIM
    if one_head_each and n_head == 4 and n_seq == 8 and block == 256:
        return half_path(queries, keys_in, values_in, out_weight, spans, full_ids)
    return ring_path(queries, keys_in, values_in, out_weight, spans, full_ids)


def solution(mesh):
    placed = (
        P("seq", "head"),
        P("seq", "head"),
        P("seq", "head"),
        P("head", None),
        P("head"),
        P("head"),
    )
    return jax.shard_map(
        on_device, mesh=mesh, in_specs=placed, out_specs=P("seq", "head"), check_vma=False
    )
```

profile of v0, /device:TPU:24, one launch (start us, length us, event | category | flops | bytes accessed | tf_op | source)
XLA Modules:
  0.0 98.5 jit_solution(2077054471009243285)
XLA Ops:
  0.1 2.5 %shard_map.64 = (bf16[1536,128]{1,0:T(8,128)(2,1)S(1)}, bf16[1536,128]{1,0:T(8,128)(2,1)S(1)}, bf16[1536,128]{1,0:T(8,128)(2,1)S(1)}, bf16[1536,128]{1,0:T(8,128...) custom-call(s32[2]{0:T(128)S(1)} %pad_add_fusion.me_ref, ...), custom_call_target="tpu_custom_call" | custom-call | flops 100000000 | bytes 1000000 | tf_op jit(solution)/shard_map/pallas_call | solution.py:416
  2.6 1.6 %collective-permute-start = (bf16[1536,128]{1,0:T(8,128)(2,1)S(1)}, bf16[1536,128]{1,0:T(8,128)(2,1)S(1)}, u32[]{:S(2)}, u32[]{:S(2)}) collective-permute-start(bf16[1536,128]{1,0:T(8,128)(2,1)S(1)} %get-tuple-element.32), channel_id=1, source_target_pairs={{0,4},{4,0},{8,12},{12,8},{16,20},{20,16},{24,28},{28,24},{1,5},{5... | collective-permute-start | bytes 1179656 | tf_op jit(solution)/shard_map/ppermute | solution.py:137
  4.6 1.5 %collective-permute-start.2 = (bf16[1536,128]{1,0:T(8,128)(2,1)S(1)}, bf16[1536,128]{1,0:T(8,128)(2,1)S(1)}, u32[]{:S(2)}, u32[]{:S(2)}) collective-permute-start(bf16[1536,128]{1,0:T(8,128)(2,1)S(1)} %get-tuple-element.34), channel_id=1, source_target_pairs={{0,12},{4,8},{8,4},{12,0},{16,28},{20,24},{24,20},{28,16},{1,13},{... | collective-permute-start | bytes 1179656 | tf_op jit(solution)/shard_map/ppermute | solution.py:137
  6.4 3.6 %collective-permute-start.7 = (bf16[256,128]{1,0:T(8,128)(2,1)S(1)}, bf16[256,128]{1,0:T(8,128)(2,1)S(1)}, u32[]{:S(2)}, u32[]{:S(2)}) collective-permute-start(bf16[256,128]{1,0:T(8,128)(2,1)S(1)} %get-tuple-element.43), channel_id=1, source_target_pairs={{0,20},{4,16},{8,28},{12,24},{16,4},{20,0},{24,12},{28,8},{1,21},{... | collective-permute-start | bytes 196616 | tf_op jit(solution)/shard_map/ppermute | solution.py:137
  10.0 4.9 %collective-permute-done.refs_1_.refs_4_ = bf16[1536,128]{1,0:T(8,128)(2,1)S(1)} collective-permute-done((bf16[1536,128]{1,0:T(8,128)(2,1)S(1)}, bf16[1536,128]{1,0:T(8,128)(2,1)S(1)}, u32[]{:S(2)}, u32[]{:S(2)}) %collective-permute-start) | collective-permute-done | bytes 393248 | tf_op jit(solution)/shard_map/ppermute | solution.py:137
  14.9 4.0 %collective-permute-done.1.refs_2_.refs_5_ = bf16[1536,128]{1,0:T(8,128)(2,1)S(1)} collective-permute-done((bf16[1536,128]{1,0:T(8,128)(2,1)S(1)}, bf16[1536,128]{1,0:T(8,128)(2,1)S(1)}, u32[]{:S(2)}, u32[]{:S(2)}) %collective-permute-start.1) | collective-permute-done | bytes 393248 | tf_op jit(solution)/shard_map/ppermute | solution.py:137
  19.7 7.3 %collective-permute-done.2.refs_3_.refs_6_ = bf16[1536,128]{1,0:T(8,128)(2,1)S(1)} collective-permute-done((bf16[1536,128]{1,0:T(8,128)(2,1)S(1)}, bf16[1536,128]{1,0:T(8,128)(2,1)S(1)}, u32[]{:S(2)}, u32[]{:S(2)}) %collective-permute-start.2) | collective-permute-done | bytes 393248 | tf_op jit(solution)/shard_map/ppermute | solution.py:137
  28.2 4.1 %shard_map.65 = (bf16[512,128]{1,0:T(8,128)(2,1)S(1)}, bf16[512,128]{1,0:T(8,128)(2,1)S(1)}, bf16[512,128]{1,0:T(8,128)(2,1)S(1)}, bf16[512,128]{1,0:T(8,128)(2,...) custom-call(s32[2]{0:T(128)S(1)} %pad_add_fusion.me_ref, ...), custom_call_target="tpu_custom_call" | custom-call | flops 2000000000 | bytes 1000000 | tf_op jit(solution)/shard_map/pallas_call | solution.py:435
  32.3 1.3 %collective-permute-start.11 = (bf16[256,128]{1,0:T(8,128)(2,1)S(1)}, bf16[256,128]{1,0:T(8,128)(2,1)S(1)}, u32[]{:S(2)}, u32[]{:S(2)}) collective-permute-start(bf16[256,128]{1,0:T(8,128)(2,1)S(1)} %get-tuple-element.50), channel_id=1, source_target_pairs={{0,20},{4,16},{8,28},{12,24},{1,21},{5,17},{9,29},{13,25},{2,22},{... | collective-permute-start | bytes 196616 | tf_op jit(solution)/shard_map/ppermute | solution.py:137
  33.6 1.3 %collective-permute-start.12 = (bf16[256,128]{1,0:T(8,128)(2,1)S(1)}, bf16[256,128]{1,0:T(8,128)(2,1)S(1)}, u32[]{:S(2)}, u32[]{:S(2)}) collective-permute-start(bf16[256,128]{1,0:T(8,128)(2,1)S(1)} %get-tuple-element.51), channel_id=1, source_target_pairs={{0,24},{4,28},{8,16},{12,20},{1,25},{5,29},{9,17},{13,21},{2,26},{... | collective-permute-start | bytes 196616 | tf_op jit(solution)/shard_map/ppermute | solution.py:137
  36.3 2.0 %shard_map.66 = (bf16[4,256,1024]{2,1,0:T(8,128)(2,1)S(1)}, f32[4,256,1]{2,1,0:T(8,128)S(1)}, f32[4,256,1]{2,1,0:T(8,128)S(1)}) custom-call(s32[2]{0:T(128)S(1)} %pad_add_fusion.me_ref, s32[8]{0:T(128)S(1)} %copy-done, s32[2]{0:T(128)S(1)} %copy-done.1, bf16[1536,128]{1,0:T(8,128)(2,1)S(1)} %get-tuple-element.31.refs_0_.refs_3_, ...), custom_call_target="tpu_custom_call" | custom-call | flops 2000000000 | bytes 1000000 | tf_op jit(solution)/shard_map/pallas_call | solution.py:451
  38.3 4.3 %collective-permute-done.11.refs_8_ = bf16[256,128]{1,0:T(8,128)(2,1)S(1)} collective-permute-done((bf16[256,128]{1,0:T(8,128)(2,1)S(1)}, bf16[256,128]{1,0:T(8,128)(2,1)S(1)}, u32[]{:S(2)}, u32[]{:S(2)}) %collective-permute-start.11) | collective-permute-done | bytes 65568 | tf_op jit(solution)/shard_map/ppermute | solution.py:137
  42.5 1.4 %collective-permute-done.13.refs_10_ = bf16[256,128]{1,0:T(8,128)(2,1)S(1)} collective-permute-done((bf16[256,128]{1,0:T(8,128)(2,1)S(1)}, bf16[256,128]{1,0:T(8,128)(2,1)S(1)}, u32[]{:S(2)}, u32[]{:S(2)}) %collective-permute-start.13) | collective-permute-done | bytes 65568 | tf_op jit(solution)/shard_map/ppermute | solution.py:137
  44.8 1.3 %collective-permute-start.14 = (bf16[272,128]{1,0:T(8,128)(2,1)S(1)}, bf16[272,128]{1,0:T(8,128)(2,1)S(1)}, u32[]{:S(2)}, u32[]{:S(2)}) collective-permute-start(bf16[272,128]{1,0:T(8,128)(2,1)S(1)} %shard_map.67.refs_8_), channel_id=1, source_target_pairs={{0,16},{4,20},{8,24},{12,28},{1,17},{5,21},{9,25},{13,29},{2,18},{... | collective-permute-start | bytes 208904 | tf_op jit(solution)/shard_map/ppermute | solution.py:137
  47.0 3.4 %collective-permute-start.18 = (bf16[272,128]{1,0:T(8,128)(2,1)S(1)}, bf16[272,128]{1,0:T(8,128)(2,1)S(1)}, u32[]{:S(2)}, u32[]{:S(2)}) collective-permute-start(bf16[272,128]{1,0:T(8,128)(2,1)S(1)} %shard_map.68), channel_id=1, source_target_pairs={{16,20},{20,16},{24,28},{28,24},{17,21},{21,17},{25,29},{29,25},{1... | collective-permute-start | bytes 208904 | tf_op jit(solution)/shard_map/ppermute | solution.py:137
  52.6 3.4 %collective-permute-start.19 = (bf16[272,128]{1,0:T(8,128)(2,1)S(1)}, bf16[272,128]{1,0:T(8,128)(2,1)S(1)}, u32[]{:S(2)}, u32[]{:S(2)}) collective-permute-start(bf16[272,128]{1,0:T(8,128)(2,1)S(1)} %shard_map.69), channel_id=1, source_target_pairs={{16,24},{20,28},{24,16},{28,20},{17,25},{21,29},{25,17},{29,21},{1... | collective-permute-start | bytes 208904 | tf_op jit(solution)/shard_map/ppermute | solution.py:137
  58.7 1.9 %collective-permute-done.15.refs_5_ = bf16[272,128]{1,0:T(8,128)(2,1)S(1)} collective-permute-done((bf16[272,128]{1,0:T(8,128)(2,1)S(1)}, bf16[272,128]{1,0:T(8,128)(2,1)S(1)}, u32[]{:S(2)}, u32[]{:S(2)}) %collective-permute-start.15) | collective-permute-done | bytes 69664 | tf_op jit(solution)/shard_map/ppermute | solution.py:137
  61.8 4.5 %collective-permute-start.20 = (bf16[272,128]{1,0:T(8,128)(2,1)S(1)}, bf16[272,128]{1,0:T(8,128)(2,1)S(1)}, u32[]{:S(2)}, u32[]{:S(2)}) collective-permute-start(bf16[272,128]{1,0:T(8,128)(2,1)S(1)} %shard_map.70), channel_id=1, source_target_pairs={{16,28},{20,24},{24,20},{28,16},{17,29},{21,25},{25,21},{29,17},{1... | collective-permute-start | bytes 208904 | tf_op jit(solution)/shard_map/ppermute | solution.py:137
  67.6 1.8 %collective-permute-done.20.refs_11_ = bf16[272,128]{1,0:T(8,128)(2,1)S(1)} collective-permute-done((bf16[272,128]{1,0:T(8,128)(2,1)S(1)}, bf16[272,128]{1,0:T(8,128)(2,1)S(1)}, u32[]{:S(2)}, u32[]{:S(2)}) %collective-permute-start.20) | collective-permute-done | bytes 69664 | tf_op jit(solution)/shard_map/ppermute | solution.py:137
  69.4 5.8 %collective-permute-done.17.refs_7_ = bf16[272,128]{1,0:T(8,128)(2,1)S(1)} collective-permute-done((bf16[272,128]{1,0:T(8,128)(2,1)S(1)}, bf16[272,128]{1,0:T(8,128)(2,1)S(1)}, u32[]{:S(2)}, u32[]{:S(2)}) %collective-permute-start.17) | collective-permute-done | bytes 69664 | tf_op jit(solution)/shard_map/ppermute | solution.py:137
  75.2 1.8 %shard_map.71.joined = bf16[256,1024]{1,0:T(8,128)(2,1)S(1)} custom-call(s32[2]{0:T(128)S(1)} %pad_add_fusion.me_ref, bf16[512,128]{1,0:T(8,128)(2,1)S(1)} %get-tuple-element.35.refs_0_, bf16[512,128]{1,0:T(8,128)(2,1)S(1)} %collective-permute-done.3.refs_1_, bf16[512,128]{1,0:T(8,128)(2,1)S(1)} %collective-permute-done.4.refs_2_, ...), custom_call_target="tpu_custom_call" | custom-call | flops 100000000 | bytes 1000000 | tf_op jit(solution)/shard_map/pallas_call | solution.py:472
  83.2 1.6 %collective-permute-start.24 = (bf16[256,512]{1,0:T(8,128)(2,1)S(1)}, bf16[256,512]{1,0:T(8,128)(2,1)S(1)}, u32[]{:S(2)}, u32[]{:S(2)}) collective-permute-start(bf16[256,512]{1,0:T(8,128)(2,1)S(1)} %add_convert_fusion.3), channel_id=1, source_target_pairs={{0,2},{1,3},{2,0},{3,1},{4,6},{5,7},{6,4},{7,5},{8,10},{9,11},{10,... | collective-permute-start | bytes 786440 | tf_op jit(solution)/shard_map/ppermute | solution.py:137
  86.5 5.9 %collective-permute-done.24 = bf16[256,512]{1,0:T(8,128)(2,1)S(1)} collective-permute-done((bf16[256,512]{1,0:T(8,128)(2,1)S(1)}, bf16[256,512]{1,0:T(8,128)(2,1)S(1)}, u32[]{:S(2)}, u32[]{:S(2)}) %collective-permute-start.24) | collective-permute-done | bytes 262176 | tf_op jit(solution)/shard_map/ppermute | solution.py:137
  92.4 5.1 %collective-permute-done.25 = bf16[256,512]{1,0:T(8,128)(2,1)S(1)} collective-permute-done((bf16[256,512]{1,0:T(8,128)(2,1)S(1)}, bf16[256,512]{1,0:T(8,128)(2,1)S(1)}, u32[]{:S(2)}, u32[]{:S(2)}) %collective-permute-start.25) | collective-permute-done | bytes 262176 | tf_op jit(solution)/shard_map/ppermute | solution.py:137
  (55 shorter events, 22.1 us)
Async XLA Ops:
  2.6 12.3 %collective-permute-start = (bf16[1536,128]{1,0:T(8,128)(2,1)S(1)}, bf16[1536,128]{1,0:T(8,128)(2,1)S(1)}, u32[]{:S(2)}, u32[]{:S(2)}) collective-permute-start(bf16[1536,128]{1,0:T(8,128)(2,1)S(1)} %get-tuple-element.32), channel_id=1, source_target_pairs={{0,4},{4,0},{8,12},{12,8},{16,20},{20,16},{24,28},{28,24},{1,5},{5... | collective-permute-start | bytes 1179656 | tf_op jit(solution)/shard_map/ppermute | solution.py:137
  4.2 14.8 %collective-permute-start.1 = (bf16[1536,128]{1,0:T(8,128)(2,1)S(1)}, bf16[1536,128]{1,0:T(8,128)(2,1)S(1)}, u32[]{:S(2)}, u32[]{:S(2)}) collective-permute-start(bf16[1536,128]{1,0:T(8,128)(2,1)S(1)} %get-tuple-element.33), channel_id=1, source_target_pairs={{0,8},{4,12},{8,0},{12,4},{16,24},{20,28},{24,16},{28,20},{1,9},{5... | collective-permute-start | bytes 1179656 | tf_op jit(solution)/shard_map/ppermute | solution.py:137
  4.6 22.3 %collective-permute-start.2 = (bf16[1536,128]{1,0:T(8,128)(2,1)S(1)}, bf16[1536,128]{1,0:T(8,128)(2,1)S(1)}, u32[]{:S(2)}, u32[]{:S(2)}) collective-permute-start(bf16[1536,128]{1,0:T(8,128)(2,1)S(1)} %get-tuple-element.34), channel_id=1, source_target_pairs={{0,12},{4,8},{8,4},{12,0},{16,28},{20,24},{24,20},{28,16},{1,13},{... | collective-permute-start | bytes 1179656 | tf_op jit(solution)/shard_map/ppermute | solution.py:137
  6.1 26.2 %collective-permute-start.6 = (bf16[256,128]{1,0:T(8,128)(2,1)S(1)}, bf16[256,128]{1,0:T(8,128)(2,1)S(1)}, u32[]{:S(2)}, u32[]{:S(2)}) collective-permute-start(bf16[256,128]{1,0:T(8,128)(2,1)S(1)} %get-tuple-element.42), channel_id=1, source_target_pairs={{0,16},{4,20},{8,24},{12,28},{16,0},{20,4},{24,8},{28,12},{1,17},{... | collective-permute-start | bytes 196616 | tf_op jit(solution)/shard_map/ppermute | solution.py:137
  6.4 27.2 %collective-permute-start.7 = (bf16[256,128]{1,0:T(8,128)(2,1)S(1)}, bf16[256,128]{1,0:T(8,128)(2,1)S(1)}, u32[]{:S(2)}, u32[]{:S(2)}) collective-permute-start(bf16[256,128]{1,0:T(8,128)(2,1)S(1)} %get-tuple-element.43), channel_id=1, source_target_pairs={{0,20},{4,16},{8,28},{12,24},{16,4},{20,0},{24,12},{28,8},{1,21},{... | collective-permute-start | bytes 196616 | tf_op jit(solution)/shard_map/ppermute | solution.py:137
  14.9 20.0 %collective-permute-start.8 = (bf16[256,128]{1,0:T(8,128)(2,1)S(1)}, bf16[256,128]{1,0:T(8,128)(2,1)S(1)}, u32[]{:S(2)}, u32[]{:S(2)}) collective-permute-start(bf16[256,128]{1,0:T(8,128)(2,1)S(1)} %get-tuple-element.44), channel_id=1, source_target_pairs={{0,24},{4,28},{8,16},{12,20},{16,8},{20,12},{24,0},{28,4},{1,25},{... | collective-permute-start | bytes 196616 | tf_op jit(solution)/shard_map/ppermute | solution.py:137
  19.0 17.3 %collective-permute-start.9 = (bf16[256,128]{1,0:T(8,128)(2,1)S(1)}, bf16[256,128]{1,0:T(8,128)(2,1)S(1)}, u32[]{:S(2)}, u32[]{:S(2)}) collective-permute-start(bf16[256,128]{1,0:T(8,128)(2,1)S(1)} %get-tuple-element.45), channel_id=1, source_target_pairs={{0,28},{4,24},{8,20},{12,16},{16,12},{20,8},{24,4},{28,0},{1,29},{... | collective-permute-start | bytes 196616 | tf_op jit(solution)/shard_map/ppermute | solution.py:137
  26.9 11.3 %collective-permute-start.10 = (bf16[256,128]{1,0:T(8,128)(2,1)S(1)}, bf16[256,128]{1,0:T(8,128)(2,1)S(1)}, u32[]{:S(2)}, u32[]{:S(2)}) collective-permute-start(bf16[256,128]{1,0:T(8,128)(2,1)S(1)} %get-tuple-element.49), channel_id=1, source_target_pairs={{0,16},{4,20},{8,24},{12,28},{1,17},{5,21},{9,25},{13,29},{2,18},{... | collective-permute-start | bytes 196616 | tf_op jit(solution)/shard_map/ppermute | solution.py:137
  32.3 10.2 %collective-permute-start.11 = (bf16[256,128]{1,0:T(8,128)(2,1)S(1)}, bf16[256,128]{1,0:T(8,128)(2,1)S(1)}, u32[]{:S(2)}, u32[]{:S(2)}) collective-permute-start(bf16[256,128]{1,0:T(8,128)(2,1)S(1)} %get-tuple-element.50), channel_id=1, source_target_pairs={{0,20},{4,16},{8,28},{12,24},{1,21},{5,17},{9,29},{13,25},{2,22},{... | collective-permute-start | bytes 196616 | tf_op jit(solution)/shard_map/ppermute | solution.py:137
  33.6 8.9 %collective-permute-start.12 = (bf16[256,128]{1,0:T(8,128)(2,1)S(1)}, bf16[256,128]{1,0:T(8,128)(2,1)S(1)}, u32[]{:S(2)}, u32[]{:S(2)}) collective-permute-start(bf16[256,128]{1,0:T(8,128)(2,1)S(1)} %get-tuple-element.51), channel_id=1, source_target_pairs={{0,24},{4,28},{8,16},{12,20},{1,25},{5,29},{9,17},{13,21},{2,26},{... | collective-permute-start | bytes 196616 | tf_op jit(solution)/shard_map/ppermute | solution.py:137
  34.9 9.0 %collective-permute-start.13 = (bf16[256,128]{1,0:T(8,128)(2,1)S(1)}, bf16[256,128]{1,0:T(8,128)(2,1)S(1)}, u32[]{:S(2)}, u32[]{:S(2)}) collective-permute-start(bf16[256,128]{1,0:T(8,128)(2,1)S(1)} %get-tuple-element.52), channel_id=1, source_target_pairs={{0,28},{4,24},{8,20},{12,16},{1,29},{5,25},{9,21},{13,17},{2,30},{... | collective-permute-start | bytes 196616 | tf_op jit(solution)/shard_map/ppermute | solution.py:137
  44.8 12.5 %collective-permute-start.14 = (bf16[272,128]{1,0:T(8,128)(2,1)S(1)}, bf16[272,128]{1,0:T(8,128)(2,1)S(1)}, u32[]{:S(2)}, u32[]{:S(2)}) collective-permute-start(bf16[272,128]{1,0:T(8,128)(2,1)S(1)} %shard_map.67.refs_8_), channel_id=1, source_target_pairs={{0,16},{4,20},{8,24},{12,28},{1,17},{5,21},{9,25},{13,29},{2,18},{... | collective-permute-start | bytes 208904 | tf_op jit(solution)/shard_map/ppermute | solution.py:137
  47.0 11.0 %collective-permute-start.18 = (bf16[272,128]{1,0:T(8,128)(2,1)S(1)}, bf16[272,128]{1,0:T(8,128)(2,1)S(1)}, u32[]{:S(2)}, u32[]{:S(2)}) collective-permute-start(bf16[272,128]{1,0:T(8,128)(2,1)S(1)} %shard_map.68), channel_id=1, source_target_pairs={{16,20},{20,16},{24,28},{28,24},{17,21},{21,17},{25,29},{29,25},{1... | collective-permute-start | bytes 208904 | tf_op jit(solution)/shard_map/ppermute | solution.py:137
  50.4 10.1 %collective-permute-start.15 = (bf16[272,128]{1,0:T(8,128)(2,1)S(1)}, bf16[272,128]{1,0:T(8,128)(2,1)S(1)}, u32[]{:S(2)}, u32[]{:S(2)}) collective-permute-start(bf16[272,128]{1,0:T(8,128)(2,1)S(1)} %shard_map.68), channel_id=1, source_target_pairs={{0,20},{4,16},{8,28},{12,24},{1,21},{5,17},{9,29},{13,25},{2,22},{... | collective-permute-start | bytes 208904 | tf_op jit(solution)/shard_map/ppermute | solution.py:137
  52.6 9.1 %collective-permute-start.19 = (bf16[272,128]{1,0:T(8,128)(2,1)S(1)}, bf16[272,128]{1,0:T(8,128)(2,1)S(1)}, u32[]{:S(2)}, u32[]{:S(2)}) collective-permute-start(bf16[272,128]{1,0:T(8,128)(2,1)S(1)} %shard_map.69), channel_id=1, source_target_pairs={{16,24},{20,28},{24,16},{28,20},{17,25},{21,29},{25,17},{29,21},{1... | collective-permute-start | bytes 208904 | tf_op jit(solution)/shard_map/ppermute | solution.py:137
  56.0 10.3 %collective-permute-start.16 = (bf16[272,128]{1,0:T(8,128)(2,1)S(1)}, bf16[272,128]{1,0:T(8,128)(2,1)S(1)}, u32[]{:S(2)}, u32[]{:S(2)}) collective-permute-start(bf16[272,128]{1,0:T(8,128)(2,1)S(1)} %shard_map.69), channel_id=1, source_target_pairs={{0,24},{4,28},{8,16},{12,20},{1,25},{5,29},{9,17},{13,21},{2,26},{... | collective-permute-start | bytes 208904 | tf_op jit(solution)/shard_map/ppermute | solution.py:137
  57.3 17.9 %collective-permute-start.3 = (bf16[512,128]{1,0:T(8,128)(2,1)S(1)}, bf16[512,128]{1,0:T(8,128)(2,1)S(1)}, u32[]{:S(2)}, u32[]{:S(2)}) collective-permute-start(bf16[512,128]{1,0:T(8,128)(2,1)S(1)} %get-tuple-element.36), channel_id=1, source_target_pairs={{0,4},{4,0},{8,12},{12,8},{16,20},{20,16},{24,28},{28,24},{1,5},{5... | collective-permute-start | bytes 393224 | tf_op jit(solution)/shard_map/ppermute | solution.py:137
  58.0 17.2 %collective-permute-start.4 = (bf16[512,128]{1,0:T(8,128)(2,1)S(1)}, bf16[512,128]{1,0:T(8,128)(2,1)S(1)}, u32[]{:S(2)}, u32[]{:S(2)}) collective-permute-start(bf16[512,128]{1,0:T(8,128)(2,1)S(1)} %get-tuple-element.37), channel_id=1, source_target_pairs={{0,8},{4,12},{8,0},{12,4},{16,24},{20,28},{24,16},{28,20},{1,9},{5... | collective-permute-start | bytes 393224 | tf_op jit(solution)/shard_map/ppermute | solution.py:137
  60.6 14.7 %collective-permute-start.5 = (bf16[512,128]{1,0:T(8,128)(2,1)S(1)}, bf16[512,128]{1,0:T(8,128)(2,1)S(1)}, u32[]{:S(2)}, u32[]{:S(2)}) collective-permute-start(bf16[512,128]{1,0:T(8,128)(2,1)S(1)} %get-tuple-element.38), channel_id=1, source_target_pairs={{0,12},{4,8},{8,4},{12,0},{16,28},{20,24},{24,20},{28,16},{1,13},{... | collective-permute-start | bytes 393224 | tf_op jit(solution)/shard_map/ppermute | solution.py:137
  61.8 7.7 %collective-permute-start.20 = (bf16[272,128]{1,0:T(8,128)(2,1)S(1)}, bf16[272,128]{1,0:T(8,128)(2,1)S(1)}, u32[]{:S(2)}, u32[]{:S(2)}) collective-permute-start(bf16[272,128]{1,0:T(8,128)(2,1)S(1)} %shard_map.70), channel_id=1, source_target_pairs={{16,28},{20,24},{24,20},{28,16},{17,29},{21,25},{25,21},{29,17},{1... | collective-permute-start | bytes 208904 | tf_op jit(solution)/shard_map/ppermute | solution.py:137
  66.3 8.9 %collective-permute-start.17 = (bf16[272,128]{1,0:T(8,128)(2,1)S(1)}, bf16[272,128]{1,0:T(8,128)(2,1)S(1)}, u32[]{:S(2)}, u32[]{:S(2)}) collective-permute-start(bf16[272,128]{1,0:T(8,128)(2,1)S(1)} %shard_map.70), channel_id=1, source_target_pairs={{0,28},{4,24},{8,20},{12,16},{1,29},{5,25},{9,21},{13,17},{2,30},{... | collective-permute-start | bytes 208904 | tf_op jit(solution)/shard_map/ppermute | solution.py:137
  83.1 14.4 %collective-permute-start.23 = (bf16[256,1024]{1,0:T(8,128)(2,1)S(1)}, bf16[256,1024]{1,0:T(8,128)(2,1)S(1)}, u32[]{:S(2)}, u32[]{:S(2)}) collective-permute-start(bf16[256,1024]{1,0:T(8,128)(2,1)S(1)} %shard_map.76), channel_id=1, source_target_pairs={{0,1},{1,0},{2,3},{3,2},{4,5},{5,4},{6,7},{7,6},{8,9},{9,8},{10,11... | collective-permute-start | bytes 1572872 | tf_op jit(solution)/shard_map/ppermute | solution.py:137
  83.2 9.2 %collective-permute-start.24 = (bf16[256,512]{1,0:T(8,128)(2,1)S(1)}, bf16[256,512]{1,0:T(8,128)(2,1)S(1)}, u32[]{:S(2)}, u32[]{:S(2)}) collective-permute-start(bf16[256,512]{1,0:T(8,128)(2,1)S(1)} %add_convert_fusion.3), channel_id=1, source_target_pairs={{0,2},{1,3},{2,0},{3,1},{4,6},{5,7},{6,4},{7,5},{8,10},{9,11},{10,... | collective-permute-start | bytes 786440 | tf_op jit(solution)/shard_map/ppermute | solution.py:137
  84.7 12.8 %collective-permute-start.25 = (bf16[256,512]{1,0:T(8,128)(2,1)S(1)}, bf16[256,512]{1,0:T(8,128)(2,1)S(1)}, u32[]{:S(2)}, u32[]{:S(2)}) collective-permute-start(bf16[256,512]{1,0:T(8,128)(2,1)S(1)} %add_convert_fusion.2), channel_id=1, source_target_pairs={{0,2},{1,3},{2,0},{3,1},{4,6},{5,7},{6,4},{7,5},{8,10},{9,11},{10,... | collective-permute-start | bytes 786440 | tf_op jit(solution)/shard_map/ppermute | solution.py:137
  (6 other events, 139.8 us)
where the time goes:
time: 98.9 us; the launch traced here: 98.5 us
  waiting for transfers between devices  42.3 us (43%)
  starting transfers between devices  34.3 us (35%)
  Pallas kernels  20.3 us (21%)
  other arithmetic  1.25 us (1%)
    ppermute x26, waiting for transfers between devices, move(): return lax.ppermute(block, axis, pairs)  42.3 us
    ppermute x26, starting transfers between devices, move(): return lax.ppermute(block, axis, pairs)  34.3 us
    pallas_call x6, Pallas kernels, columns_of(): own_kernel(functools.partial(project, flip, part, parts), [shape((block,...  6.43 us
    pallas_call x1, Pallas kernels, half_path(): own_kernel(functools.partial(attend_own_half, half), [shape((2 * block, H...  4.05 us
    pallas_call x4, Pallas kernels, half_path(): own_kernel(functools.partial(attend_across, half, flip), [shape((block +...  3.52 us
    pallas_call x1, Pallas kernels, half_path(): own_kernel(functools.partial(deal, half), [shape((6 * block, HEAD_DIM), b...  2.49 us
    pallas_call x1, Pallas kernels, half_path(): own_kernel(functools.partial(weigh_across, half), [shape((half, block, ha...  2.01 us
  transfers between devices with their start and end apart: 26, of which 10 were waited for; matrix products, arithmetic and copies ran while one was open for 0% of the time, Pallas kernels for 13%

commit v1 on v0

--- a/solution.py
+++ b/solution.py
@@ -254,10 +254,9 @@
 
 
 def attend_own_half(half, me_ref, *refs):
-    inner, out_refs = refs[:half], refs[half : 2 * half]
-    num_ref, total_ref, peak_ref, qkv, o_low, o_up, stats = refs[2 * half :]
+    inner, (o_low, o_up, stat_ref, num_ref, total_ref, peak_ref, qkv) = refs[:half], refs[half:]
     low = me_ref[0] % half
-    block = out_refs[0].shape[0] // 2
+    block = o_low.shape[1]
     for flip in range(half):
         at = pl.multiple_of((low ^ flip) * block, block)
         for place in range(6):
@@ -276,22 +275,12 @@
             result = (numerator / total).astype(jnp.bfloat16)
             if head == 0:
                 o_low[i] = result
-                stats[i] = pack_stat(peak * FACTOR + jnp.log2(total))
+                stat_ref[i] = pack_stat(peak * FACTOR + jnp.log2(total))
             else:
                 o_up[i] = result
                 num_ref[i] = numerator
                 total_ref[i] = total
                 peak_ref[i] = peak
-    for flip in range(half):
-        out_refs[flip][:block] = o_low[low ^ flip]
-
-        @pl.when(me_ref[0] < half)
-        def _():
-            out_refs[flip][block:] = o_up[low ^ flip]
-
-        @pl.when(me_ref[0] >= half)
-        def _():
-            out_refs[flip][block : block + STAT_ROWS] = stats[low ^ flip]
 
 
 def weigh_across(half, me_ref, spans_ref, full_ref, *refs):
@@ -336,13 +325,17 @@
         peak_ref[flip] = peak
 
 
-def attend_across(half, flip, me_ref, num_ref, total_ref, peak_ref, *refs):
-    weight_ref, far_total_ref, far_peak_ref = refs[:3]
-    inner, cross_v = refs[3 : 3 + half], refs[3 + half : 3 + 2 * half]
-    out_ref, values = refs[3 + 2 * half :]
+def attend_across(half, flip, me_ref, *refs):
+    o_low, o_up, stat_ref, num_ref, total_ref, peak_ref = refs[:6]
+    weight_ref, far_total_ref, far_peak_ref = refs[6:9]
+    inner, cross_v = refs[9 : 9 + half], refs[9 + half : 9 + 2 * half]
+    across_ref, inner_ref, values = refs[9 + 2 * half :]
     me = me_ref[0]
-    block = out_ref.shape[0] - STAT_ROWS
+    block = o_low.shape[1]
     below = me < half
+    row_block = me % half ^ flip
+    inner_ref[:block] = o_low[row_block]
+    inner_ref[2 * block :] = stat_ref[row_block]
 
     @pl.when(below)
     def _():
@@ -355,49 +348,57 @@
             values[other * block : (other + 1) * block] = cross_v[other][...]
 
     numerator = jnp.dot(weight_ref[flip], values[...], preferred_element_type=jnp.float32)
-    row_block = me % half ^ flip
     total, peak = far_total_ref[flip], far_peak_ref[flip]
-    own_peak = jnp.where(below, NEG_FILL, peak_ref[row_block])
-    joint = jnp.maximum(peak, own_peak)
-    scale = jnp.exp2((peak - joint) * FACTOR)
-    own_scale = jnp.where(below, 0.0, jnp.exp2((own_peak - joint) * FACTOR))
-    numerator = numerator * scale + num_ref[row_block] * own_scale
-    total = total * scale + total_ref[row_block] * own_scale
-    out_ref[:block] = (numerator / total).astype(jnp.bfloat16)
-    out_ref[block:] = pack_stat(joint * FACTOR + jnp.log2(total))
-
-
-def join_heads(half, me_ref, *refs):
-    own, across, upper = refs[:half], refs[half : 2 * half], refs[2 * half : 3 * half]
-    joined = refs[3 * half]
+
+    @pl.when(below)
+    def _():
+        across_ref[:block] = (numerator / total).astype(jnp.bfloat16)
+        across_ref[block:] = pack_stat(peak * FACTOR + jnp.log2(total))
+        inner_ref[block : 2 * block] = o_up[row_block]
+
+    @pl.when(jnp.logical_not(below))
+    def _():
+        own_peak = peak_ref[row_block]
+        joint = jnp.maximum(peak, own_peak)
+        scale = jnp.exp2((peak - joint) * FACTOR)
+        own_scale = jnp.exp2((own_peak - joint) * FACTOR)
+        both = numerator * scale + num_ref[row_block] * own_scale
+        both_total = total * scale + total_ref[row_block] * own_scale
+        inner_ref[block : 2 * block] = (both / both_total).astype(jnp.bfloat16)
+
+
+def join_heads(half, me_ref, inner, across, joined):
     me = me_ref[0]
     low = me % half
     block = joined.shape[0]
     for flip in range(half):
         at = pl.multiple_of((low ^ flip) * HEAD_DIM, HEAD_DIM)
         up_at = pl.multiple_of((low ^ flip) * HEAD_DIM + half * HEAD_DIM, HEAD_DIM)
+        joined[:, pl.ds(up_at, HEAD_DIM)] = inner[flip][block : 2 * block]
 
         @pl.when(me < half)
         def _():
-            joined[:, pl.ds(at, HEAD_DIM)] = own[flip][:block]
-            joined[:, pl.ds(up_at, HEAD_DIM)] = own[flip][block:]
+            joined[:, pl.ds(at, HEAD_DIM)] = inner[flip][:block]
 
         @pl.when(me >= half)
         def _():
-            here = unpack_stat(own[flip][block : block + STAT_ROWS], block)
+            here = unpack_stat(inner[flip][2 * block :], block)
             there = unpack_stat(across[flip][block:], block)
-            joint = jnp.maximum(here, there)
-            here, there = jnp.exp2(here - joint), jnp.exp2(there - joint)
-            total = here + there
-            mixed = own[flip][:block].astype(jnp.float32) * (here / total)
-            mixed = mixed + across[flip][:block].astype(jnp.float32) * (there / total)
+            share = 1.0 / (1.0 + jnp.exp2(there - here))
+            mixed = inner[flip][:block].astype(jnp.float32) * share
+            mixed = mixed + across[flip][:block].astype(jnp.float32) * (1.0 - share)
             joined[:, pl.ds(at, HEAD_DIM)] = mixed.astype(jnp.bfloat16)
-            joined[:, pl.ds(up_at, HEAD_DIM)] = upper[flip][:block]
-
-
-def project(flip, part, parts, me_ref, joined, w_ref, out_ref):
+
+
+def join_and_project(half, flip, me_ref, *refs):
+    inner, across, (w_ref, out_ref, joined) = refs[:half], refs[half : 2 * half], refs[2 * half :]
+    join_heads(half, me_ref, inner, across, joined)
+    project(flip, me_ref, joined, w_ref, out_ref)
+
+
+def project(flip, me_ref, joined, w_ref, out_ref):
     width = out_ref.shape[1]
-    at = pl.multiple_of(((me_ref[1] ^ flip) * parts + part) * width, width)
+    at = pl.multiple_of((me_ref[1] ^ flip) * width, width)
     out_ref[...] = jnp.dot(
         joined[...], w_ref[:, pl.ds(at, width)], preferred_element_type=jnp.float32
     ).astype(jnp.bfloat16)
@@ -432,22 +433,15 @@
     cross = [held(a) for a in cross]
     cross_v = [held(a) for a in cross_v]
 
-    *own, numerator, total, peak = own_kernel(
+    own = own_kernel(
         functools.partial(attend_own_half, half),
-        [shape((2 * block, HEAD_DIM), bf16)] * half
-        + [shape((half, block, HEAD_DIM), f32)]
+        [shape((half, block, HEAD_DIM), bf16)] * 2
+        + [shape((half, STAT_ROWS, HEAD_DIM), bf16), shape((half, block, HEAD_DIM), f32)]
         + [shape((half, block, 1), f32)] * 2,
         [SMEM] + in_vmem(half),
-        [
-            pltpu.VMEM((6, half * block, HEAD_DIM), bf16),
-            pltpu.VMEM((half, block, HEAD_DIM), bf16),
-            pltpu.VMEM((half, block, HEAD_DIM), bf16),
-            pltpu.VMEM((half, STAT_ROWS, HEAD_DIM), bf16),
-        ],
+        [pltpu.VMEM((6, half * block, HEAD_DIM), bf16)],
         flops=2 * 10**9,
     )(where, *inner)
-    for flip in range(half - 1, 0, -1):
-        own[flip] = swap(own[flip], "seq", flip)
     weights = own_kernel(
         functools.partial(weigh_across, half),
         [shape((half, block, half * block), bf16)] + [shape((half, block, 1), f32)] * 2,
@@ -455,52 +449,45 @@
         [pltpu.VMEM((half, block, HEAD_DIM), bf16)] * 2,
         flops=2 * 10**9,
     )(where, spans, full_ids, *inner, *cross)
-    state = [held(a) for a in (numerator, total, peak, *weights)]
-    across, upper = [None] * half, [None] * half
-    for flip in down:
-        (sent,) = own_kernel(
+    state = [held(a) for a in (*own, *weights)]
+    across, own_half = [None] * half, [None] * half
+    for flip in range(half):
+        far, near = own_kernel(
             functools.partial(attend_across, half, flip),
-            [shape((block + STAT_ROWS, HEAD_DIM), bf16)],
-            [SMEM] + in_vmem(6 + 2 * half),
+            [
+                shape((block + STAT_ROWS, HEAD_DIM), bf16),
+                shape((2 * block + STAT_ROWS, HEAD_DIM), bf16),
+            ],
+            [SMEM] + in_vmem(len(state) + 2 * half),
             [pltpu.VMEM((half * block, HEAD_DIM), bf16)],
             flops=5 * 10**8,
         )(where, *state, *inner, *cross_v)
-        across[flip] = move(sent, "seq", [(i, half + (i ^ flip)) for i in range(half)])
-        upper[flip] = sent
-        if flip:
-            upper[flip] = move(sent, "seq", [(half + i, half + (i ^ flip)) for i in range(half)])
-    (joined,) = own_kernel(
-        functools.partial(join_heads, half),
-        [shape((block, n_seq * HEAD_DIM), bf16)],
-        [SMEM] + in_vmem(3 * half),
-    )(where, *[held(a) for a in own + across + upper])
-    joined = held(joined)
-
+        across[flip] = move(far, "seq", [(i, half + (i ^ flip)) for i in range(half)])
+        own_half[flip] = swap(near, "seq", flip) if flip else near
+    came = [held(a) for a in own_half + across]
     width = out_weight.shape[1] // lax.axis_size("head")
-
-    def columns_of(flip, part, parts, rows):
+    part = shape((block, width), bf16)
+    sent, joined = own_kernel(
+        functools.partial(join_and_project, half, 3),
+        [part, shape((block, n_seq * HEAD_DIM), bf16)],
+        [SMEM] + in_vmem(2 * half + 1),
+        flops=10**9,
+    )(where, *came, w_held)
+
+    def columns_of(flip, rows):
         return own_kernel(
-            functools.partial(project, flip, part, parts),
-            [shape((block, width // parts), bf16)],
-            [SMEM] + in_vmem(2),
-            flops=10**9 // parts,
-        )(where, rows, w_held)[0]
-
-    def summed(came, kept):
-        return (came.astype(f32) + kept.astype(f32)).astype(bf16)
-
-    parts = 2
-    sent = [columns_of(3, part, parts, joined) for part in range(parts)]
-    came = [swap(a, "head", 1) for a in sent]
-    rows, _ = lax.optimization_barrier((joined, sent[-1]))
-    kept = [columns_of(2, part, parts, held(rows)) for part in range(parts)]
-    far = [summed(a, b) for a, b in zip(came, kept)]
-    rows, *far = lax.optimization_barrier((joined, *far))
-    far = [swap(a, "head", 2) for a in far]
-    near = columns_of(1, 0, 1, held(rows))
-    near = swap(near, "head", 1)
-    near = summed(near, columns_of(0, 0, 1, held(rows)))
-    return (near.astype(f32) + jnp.concatenate(far, axis=1).astype(f32)).astype(bf16)
+            functools.partial(project, flip), [part], [SMEM] + in_vmem(2), flops=10**9
+        )(where, held(rows), w_held)[0]
+
+    def summed(one, other):
+        return (one.astype(f32) + other.astype(f32)).astype(bf16)
+
+    far = summed(swap(sent, "head", 1), columns_of(2, joined))
+    rows, far = lax.optimization_barrier((joined, far))
+    far = swap(far, "head", 2)
+    near = columns_of(1, rows)
+    near = summed(swap(near, "head", 1), columns_of(0, rows))
+    return summed(near, far)
 
 
 def on_device(queries, keys_in, values_in, out_weight, spans, full_ids):

time: 98.9 us -> 89.7 us (0.907)
  the two profiles are of different devices: /device:TPU:24 before, /device:TPU:0 now
where the time goes in v1:
time: 89.7 us; the launch traced here: 89.1 us
  starting transfers between devices  48.1 us (54%)
  waiting for transfers between devices  21.6 us (24%)
  Pallas kernels  17.7 us (20%)
  other arithmetic  1.33 us (1%)
    ppermute x21, starting transfers between devices, move(): return lax.ppermute(block, axis, pairs)  48.1 us
    ppermute x21, waiting for transfers between devices, move(): return lax.ppermute(block, axis, pairs)  21.6 us
    pallas_call x4, Pallas kernels, half_path(): own_kernel(functools.partial(attend_across, half, flip), [shape((block +...  4.06 us
    pallas_call x1, Pallas kernels, half_path(): own_kernel(functools.partial(attend_own_half, half), [shape((half, block,...  4 us
    pallas_call x3, Pallas kernels, columns_of(): own_kernel(functools.partial(project, flip), [part], [SMEM] + in_vmem(2),...  3.76 us
    pallas_call x1, Pallas kernels, half_path(): own_kernel(functools.partial(deal, half), [shape((6 * block, HEAD_DIM), b...  2.45 us
    pallas_call x1, Pallas kernels, half_path(): own_kernel(functools.partial(weigh_across, half), [shape((half, block, ha...  2.01 us
  transfers between devices with their start and end apart: 21, of which 6 were waited for; matrix products, arithmetic and copies ran while one was open for 0% of the time, Pallas kernels for 13%

profile of v1, /device:TPU:0, one launch (start us, length us, event | category | flops | bytes accessed | tf_op | source)
XLA Modules:
  0.0 89.1 jit_solution(6306734341525955370)
XLA Ops:
  0.1 2.5 %shard_map.64 = (bf16[1536,128]{1,0:T(8,128)(2,1)S(1)}, bf16[1536,128]{1,0:T(8,128)(2,1)S(1)}, bf16[1536,128]{1,0:T(8,128)(2,1)S(1)}, bf16[1536,128]{1,0:T(8,128...) custom-call(s32[2]{0:T(128)S(1)} %pad_add_fusion.me_ref, ...), custom_call_target="tpu_custom_call" | custom-call | flops 100000000 | bytes 1000000 | tf_op jit(solution)/shard_map/pallas_call | solution.py:417
  2.5 3.1 %collective-permute-start = (bf16[1536,128]{1,0:T(8,128)(2,1)S(1)}, bf16[1536,128]{1,0:T(8,128)(2,1)S(1)}, u32[]{:S(2)}, u32[]{:S(2)}) collective-permute-start(bf16[1536,128]{1,0:T(8,128)(2,1)S(1)} %get-tuple-element.39), channel_id=1, source_target_pairs={{0,4},{4,0},{8,12},{12,8},{16,20},{20,16},{24,28},{28,24},{1,5},{5... | collective-permute-start | bytes 1179656 | tf_op jit(solution)/shard_map/ppermute | solution.py:137
  5.6 1.6 %collective-permute-start.1 = (bf16[1536,128]{1,0:T(8,128)(2,1)S(1)}, bf16[1536,128]{1,0:T(8,128)(2,1)S(1)}, u32[]{:S(2)}, u32[]{:S(2)}) collective-permute-start(bf16[1536,128]{1,0:T(8,128)(2,1)S(1)} %get-tuple-element.40), channel_id=1, source_target_pairs={{0,8},{4,12},{8,0},{12,4},{16,24},{20,28},{24,16},{28,20},{1,9},{5... | collective-permute-start | bytes 1179656 | tf_op jit(solution)/shard_map/ppermute | solution.py:137
  7.2 3.0 %collective-permute-start.3 = (bf16[256,128]{1,0:T(8,128)(2,1)S(1)}, bf16[256,128]{1,0:T(8,128)(2,1)S(1)}, u32[]{:S(2)}, u32[]{:S(2)}) collective-permute-start(bf16[256,128]{1,0:T(8,128)(2,1)S(1)} %get-tuple-element.48), channel_id=1, source_target_pairs={{0,16},{4,20},{8,24},{12,28},{16,0},{20,4},{24,8},{28,12},{1,17},{... | collective-permute-start | bytes 196616 | tf_op jit(solution)/shard_map/ppermute | solution.py:137
  10.2 1.3 %collective-permute-start.4 = (bf16[256,128]{1,0:T(8,128)(2,1)S(1)}, bf16[256,128]{1,0:T(8,128)(2,1)S(1)}, u32[]{:S(2)}, u32[]{:S(2)}) collective-permute-start(bf16[256,128]{1,0:T(8,128)(2,1)S(1)} %get-tuple-element.49), channel_id=1, source_target_pairs={{0,20},{4,16},{8,28},{12,24},{16,4},{20,0},{24,12},{28,8},{1,21},{... | collective-permute-start | bytes 196616 | tf_op jit(solution)/shard_map/ppermute | solution.py:137
  11.5 4.0 %collective-permute-done.refs_1_.refs_10_ = bf16[1536,128]{1,0:T(8,128)(2,1)S(1)} collective-permute-done((bf16[1536,128]{1,0:T(8,128)(2,1)S(1)}, bf16[1536,128]{1,0:T(8,128)(2,1)S(1)}, u32[]{:S(2)}, u32[]{:S(2)}) %collective-permute-start) | collective-permute-done | bytes 393248 | tf_op jit(solution)/shard_map/ppermute | solution.py:137
  15.4 4.6 %collective-permute-start.5 = (bf16[256,128]{1,0:T(8,128)(2,1)S(1)}, bf16[256,128]{1,0:T(8,128)(2,1)S(1)}, u32[]{:S(2)}, u32[]{:S(2)}) collective-permute-start(bf16[256,128]{1,0:T(8,128)(2,1)S(1)} %get-tuple-element.50), channel_id=1, source_target_pairs={{0,24},{4,28},{8,16},{12,20},{16,8},{20,12},{24,0},{28,4},{1,25},{... | collective-permute-start | bytes 196616 | tf_op jit(solution)/shard_map/ppermute | solution.py:137
  20.4 3.6 %collective-permute-start.6 = (bf16[256,128]{1,0:T(8,128)(2,1)S(1)}, bf16[256,128]{1,0:T(8,128)(2,1)S(1)}, u32[]{:S(2)}, u32[]{:S(2)}) collective-permute-start(bf16[256,128]{1,0:T(8,128)(2,1)S(1)} %get-tuple-element.51), channel_id=1, source_target_pairs={{0,28},{4,24},{8,20},{12,16},{16,12},{20,8},{24,4},{28,0},{1,29},{... | collective-permute-start | bytes 196616 | tf_op jit(solution)/shard_map/ppermute | solution.py:137
  24.0 3.2 %collective-permute-done.2.refs_3_.refs_12_ = bf16[1536,128]{1,0:T(8,128)(2,1)S(1)} collective-permute-done((bf16[1536,128]{1,0:T(8,128)(2,1)S(1)}, bf16[1536,128]{1,0:T(8,128)(2,1)S(1)}, u32[]{:S(2)}, u32[]{:S(2)}) %collective-permute-start.2) | collective-permute-done | bytes 393248 | tf_op jit(solution)/shard_map/ppermute | solution.py:137
  27.2 7.4 %collective-permute-start.10 = (bf16[256,128]{1,0:T(8,128)(2,1)S(1)}, bf16[256,128]{1,0:T(8,128)(2,1)S(1)}, u32[]{:S(2)}, u32[]{:S(2)}) collective-permute-start(bf16[256,128]{1,0:T(8,128)(2,1)S(1)} %get-tuple-element.58), channel_id=1, source_target_pairs={{0,28},{4,24},{8,20},{12,16},{1,29},{5,25},{9,21},{13,17},{2,30},{... | collective-permute-start | bytes 196616 | tf_op jit(solution)/shard_map/ppermute | solution.py:137
  34.6 4.0 %shard_map.65 = (bf16[4,256,128]{2,1,0:T(8,128)(2,1)S(1)}, bf16[4,256,128]{2,1,0:T(8,128)(2,1)S(1)}, bf16[4,16,128]{2,1,0:T(8,128)(2,1)S(1)}, f32[4,256,128]{2,1...) custom-call(s32[2]{0:T(128)S(1)} %pad_add_fusion.me_ref, ...), custom_call_target="tpu_custom_call" | custom-call | flops 2000000000 | bytes 1000000 | tf_op jit(solution)/shard_map/pallas_call | solution.py:436
  38.7 1.3 %collective-permute-start.7 = (bf16[256,128]{1,0:T(8,128)(2,1)S(1)}, bf16[256,128]{1,0:T(8,128)(2,1)S(1)}, u32[]{:S(2)}, u32[]{:S(2)}) collective-permute-start(bf16[256,128]{1,0:T(8,128)(2,1)S(1)} %get-tuple-element.55), channel_id=1, source_target_pairs={{0,16},{4,20},{8,24},{12,28},{1,17},{5,21},{9,25},{13,29},{2,18},{... | collective-permute-start | bytes 196616 | tf_op jit(solution)/shard_map/ppermute | solution.py:137
  40.0 1.3 %collective-permute-start.8 = (bf16[256,128]{1,0:T(8,128)(2,1)S(1)}, bf16[256,128]{1,0:T(8,128)(2,1)S(1)}, u32[]{:S(2)}, u32[]{:S(2)}) collective-permute-start(bf16[256,128]{1,0:T(8,128)(2,1)S(1)} %get-tuple-element.56), channel_id=1, source_target_pairs={{0,20},{4,16},{8,28},{12,24},{1,21},{5,17},{9,29},{13,25},{2,22},{... | collective-permute-start | bytes 196616 | tf_op jit(solution)/shard_map/ppermute | solution.py:137
  41.3 1.3 %collective-permute-start.9 = (bf16[256,128]{1,0:T(8,128)(2,1)S(1)}, bf16[256,128]{1,0:T(8,128)(2,1)S(1)}, u32[]{:S(2)}, u32[]{:S(2)}) collective-permute-start(bf16[256,128]{1,0:T(8,128)(2,1)S(1)} %get-tuple-element.57), channel_id=1, source_target_pairs={{0,24},{4,28},{8,16},{12,20},{1,25},{5,29},{9,17},{13,21},{2,26},{... | collective-permute-start | bytes 196616 | tf_op jit(solution)/shard_map/ppermute | solution.py:137
  42.6 2.0 %shard_map.66 = (bf16[4,256,1024]{2,1,0:T(8,128)(2,1)S(1)}, f32[4,256,1]{2,1,0:T(8,128)S(1)}, f32[4,256,1]{2,1,0:T(8,128)S(1)}) custom-call(s32[2]{0:T(128)S(1)} %pad_add_fusion.me_ref, s32[8]{0:T(128)S(1)} %copy-done, s32[2]{0:T(128)S(1)} %copy-done.1, bf16[1536,128]{1,0:T(8,128)(2,1)S(1)} %get-tuple-element.38.refs_0_.refs_9_, ...), custom_call_target="tpu_custom_call" | custom-call | flops 2000000000 | bytes 1000000 | tf_op jit(solution)/shard_map/pallas_call | solution.py:445
  45.7 2.5 %collective-permute-start.13 = (bf16[528,128]{1,0:T(8,128)(2,1)S(1)}, bf16[528,128]{1,0:T(8,128)(2,1)S(1)}, u32[]{:S(2)}, u32[]{:S(2)}) collective-permute-start(bf16[528,128]{1,0:T(8,128)(2,1)S(1)} %get-tuple-element.62), channel_id=1, source_target_pairs={{0,12},{4,8},{8,4},{12,0},{16,28},{20,24},{24,20},{28,16},{1,13},{... | collective-permute-start | bytes 405512 | tf_op jit(solution)/shard_map/ppermute | solution.py:137
  48.2 6.3 %collective-permute-start.17 = (bf16[272,128]{1,0:T(8,128)(2,1)S(1)}, bf16[272,128]{1,0:T(8,128)(2,1)S(1)}, u32[]{:S(2)}, u32[]{:S(2)}) collective-permute-start(bf16[272,128]{1,0:T(8,128)(2,1)S(1)} %get-tuple-element.66), channel_id=1, source_target_pairs={{0,28},{4,24},{8,20},{12,16},{1,29},{5,25},{9,21},{13,17},{2,30},{... | collective-permute-start | bytes 208904 | tf_op jit(solution)/shard_map/ppermute | solution.py:137
  55.6 2.3 %collective-permute-start.16 = (bf16[272,128]{1,0:T(8,128)(2,1)S(1)}, bf16[272,128]{1,0:T(8,128)(2,1)S(1)}, u32[]{:S(2)}, u32[]{:S(2)}) collective-permute-start(bf16[272,128]{1,0:T(8,128)(2,1)S(1)} %get-tuple-element.65), channel_id=1, source_target_pairs={{0,24},{4,28},{8,16},{12,20},{1,25},{5,29},{9,17},{13,21},{2,26},{... | collective-permute-start | bytes 208904 | tf_op jit(solution)/shard_map/ppermute | solution.py:137
  60.7 1.3 %collective-permute-start.15 = (bf16[272,128]{1,0:T(8,128)(2,1)S(1)}, bf16[272,128]{1,0:T(8,128)(2,1)S(1)}, u32[]{:S(2)}, u32[]{:S(2)}) collective-permute-start(bf16[272,128]{1,0:T(8,128)(2,1)S(1)} %get-tuple-element.64), channel_id=1, source_target_pairs={{0,20},{4,16},{8,28},{12,24},{1,21},{5,17},{9,29},{13,25},{2,22},{... | collective-permute-start | bytes 208904 | tf_op jit(solution)/shard_map/ppermute | solution.py:137
  62.0 4.8 %collective-permute-start.14 = (bf16[272,128]{1,0:T(8,128)(2,1)S(1)}, bf16[272,128]{1,0:T(8,128)(2,1)S(1)}, u32[]{:S(2)}, u32[]{:S(2)}) collective-permute-start(bf16[272,128]{1,0:T(8,128)(2,1)S(1)} %get-tuple-element.63), channel_id=1, source_target_pairs={{0,16},{4,20},{8,24},{12,28},{1,17},{5,21},{9,25},{13,29},{2,18},{... | collective-permute-start | bytes 208904 | tf_op jit(solution)/shard_map/ppermute | solution.py:137
  66.8 1.9 %collective-permute-done.14.refs_4_ = bf16[272,128]{1,0:T(8,128)(2,1)S(1)} collective-permute-done((bf16[272,128]{1,0:T(8,128)(2,1)S(1)}, bf16[272,128]{1,0:T(8,128)(2,1)S(1)}, u32[]{:S(2)}, u32[]{:S(2)}) %collective-permute-start.14) | collective-permute-done | bytes 69664 | tf_op jit(solution)/shard_map/ppermute | solution.py:137
  68.8 1.4 %shard_map.71 = (bf16[256,1024]{1,0:T(8,128)(2,1)S(1)}, bf16[256,1024]{1,0:T(8,128)(2,1)S(1)}) custom-call(s32[2]{0:T(128)S(1)} %pad_add_fusion.me_ref, bf16[528,128]{1,0:T(8,128)(2,1)S(1)} %get-tuple-element.59.refs_0_, bf16[528,128]{1,0:T(8,128)(2,1)S(1)} %collective-permute-done.11.refs_1_, bf16[528,128]{1,0:T(8,128)(2,1)S(1)} %collective-permute-done.12.refs_2_, ...), custom_call_target="tpu_custom_call" | custom-call | flops 1000000000 | bytes 1000000 | tf_op jit(solution)/shard_map/pallas_call | solution.py:470
  73.8 1.5 %collective-permute-start.20 = (bf16[256,1024]{1,0:T(8,128)(2,1)S(1)}, bf16[256,1024]{1,0:T(8,128)(2,1)S(1)}, u32[]{:S(2)}, u32[]{:S(2)}) collective-permute-start(bf16[256,1024]{1,0:T(8,128)(2,1)S(1)} %add_convert_fusion.2), channel_id=1, source_target_pairs={{0,2},{1,3},{2,0},{3,1},{4,6},{5,7},{6,4},{7,5},{8,10},{9,11},{10,... | collective-permute-start | bytes 1572872 | tf_op jit(solution)/shard_map/ppermute | solution.py:137
  76.6 11.4 %collective-permute-done.20 = bf16[256,1024]{1,0:T(8,128)(2,1)S(1)} collective-permute-done((bf16[256,1024]{1,0:T(8,128)(2,1)S(1)}, bf16[256,1024]{1,0:T(8,128)(2,1)S(1)}, u32[]{:S(2)}, u32[]{:S(2)}) %collective-permute-start.20) | collective-permute-done | bytes 524320 | tf_op jit(solution)/shard_map/ppermute | solution.py:137
  (41 shorter events, 11.3 us)
Async XLA Ops:
  0.0 42.6 %copy-start = (s32[8]{0:T(128)S(1)}, s32[8]{0:T(128)}, u32[]{:S(2)}) copy-start(s32[8]{0:T(128)} %spans_ref.1) | copy-start | bytes 100
  0.0 42.6 %copy-start.1 = (s32[2]{0:T(128)S(1)}, s32[2]{0:T(128)}, u32[]{:S(2)}) copy-start(s32[2]{0:T(128)} %full_ref.1) | copy-start | bytes 28
  2.5 12.9 %collective-permute-start = (bf16[1536,128]{1,0:T(8,128)(2,1)S(1)}, bf16[1536,128]{1,0:T(8,128)(2,1)S(1)}, u32[]{:S(2)}, u32[]{:S(2)}) collective-permute-start(bf16[1536,128]{1,0:T(8,128)(2,1)S(1)} %get-tuple-element.39), channel_id=1, source_target_pairs={{0,4},{4,0},{8,12},{12,8},{16,20},{20,16},{24,28},{28,24},{1,5},{5... | collective-permute-start | bytes 1179656 | tf_op jit(solution)/shard_map/ppermute | solution.py:137
  5.6 14.8 %collective-permute-start.1 = (bf16[1536,128]{1,0:T(8,128)(2,1)S(1)}, bf16[1536,128]{1,0:T(8,128)(2,1)S(1)}, u32[]{:S(2)}, u32[]{:S(2)}) collective-permute-start(bf16[1536,128]{1,0:T(8,128)(2,1)S(1)} %get-tuple-element.40), channel_id=1, source_target_pairs={{0,8},{4,12},{8,0},{12,4},{16,24},{20,28},{24,16},{28,20},{1,9},{5... | collective-permute-start | bytes 1179656 | tf_op jit(solution)/shard_map/ppermute | solution.py:137
  7.2 20.0 %collective-permute-start.2 = (bf16[1536,128]{1,0:T(8,128)(2,1)S(1)}, bf16[1536,128]{1,0:T(8,128)(2,1)S(1)}, u32[]{:S(2)}, u32[]{:S(2)}) collective-permute-start(bf16[1536,128]{1,0:T(8,128)(2,1)S(1)} %get-tuple-element.41), channel_id=1, source_target_pairs={{0,12},{4,8},{8,4},{12,0},{16,28},{20,24},{24,20},{28,16},{1,13},{... | collective-permute-start | bytes 1179656 | tf_op jit(solution)/shard_map/ppermute | solution.py:137
  7.2 31.5 %collective-permute-start.3 = (bf16[256,128]{1,0:T(8,128)(2,1)S(1)}, bf16[256,128]{1,0:T(8,128)(2,1)S(1)}, u32[]{:S(2)}, u32[]{:S(2)}) collective-permute-start(bf16[256,128]{1,0:T(8,128)(2,1)S(1)} %get-tuple-element.48), channel_id=1, source_target_pairs={{0,16},{4,20},{8,24},{12,28},{16,0},{20,4},{24,8},{28,12},{1,17},{... | collective-permute-start | bytes 196616 | tf_op jit(solution)/shard_map/ppermute | solution.py:137
  10.2 29.8 %collective-permute-start.4 = (bf16[256,128]{1,0:T(8,128)(2,1)S(1)}, bf16[256,128]{1,0:T(8,128)(2,1)S(1)}, u32[]{:S(2)}, u32[]{:S(2)}) collective-permute-start(bf16[256,128]{1,0:T(8,128)(2,1)S(1)} %get-tuple-element.49), channel_id=1, source_target_pairs={{0,20},{4,16},{8,28},{12,24},{16,4},{20,0},{24,12},{28,8},{1,21},{... | collective-permute-start | bytes 196616 | tf_op jit(solution)/shard_map/ppermute | solution.py:137
  15.4 25.9 %collective-permute-start.5 = (bf16[256,128]{1,0:T(8,128)(2,1)S(1)}, bf16[256,128]{1,0:T(8,128)(2,1)S(1)}, u32[]{:S(2)}, u32[]{:S(2)}) collective-permute-start(bf16[256,128]{1,0:T(8,128)(2,1)S(1)} %get-tuple-element.50), channel_id=1, source_target_pairs={{0,24},{4,28},{8,16},{12,20},{16,8},{20,12},{24,0},{28,4},{1,25},{... | collective-permute-start | bytes 196616 | tf_op jit(solution)/shard_map/ppermute | solution.py:137
  20.4 22.2 %collective-permute-start.6 = (bf16[256,128]{1,0:T(8,128)(2,1)S(1)}, bf16[256,128]{1,0:T(8,128)(2,1)S(1)}, u32[]{:S(2)}, u32[]{:S(2)}) collective-permute-start(bf16[256,128]{1,0:T(8,128)(2,1)S(1)} %get-tuple-element.51), channel_id=1, source_target_pairs={{0,28},{4,24},{8,20},{12,16},{16,12},{20,8},{24,4},{28,0},{1,29},{... | collective-permute-start | bytes 196616 | tf_op jit(solution)/shard_map/ppermute | solution.py:137
  27.2 17.4 %collective-permute-start.10 = (bf16[256,128]{1,0:T(8,128)(2,1)S(1)}, bf16[256,128]{1,0:T(8,128)(2,1)S(1)}, u32[]{:S(2)}, u32[]{:S(2)}) collective-permute-start(bf16[256,128]{1,0:T(8,128)(2,1)S(1)} %get-tuple-element.58), channel_id=1, source_target_pairs={{0,28},{4,24},{8,20},{12,16},{1,29},{5,25},{9,21},{13,17},{2,30},{... | collective-permute-start | bytes 196616 | tf_op jit(solution)/shard_map/ppermute | solution.py:137
  38.7 6.0 %collective-permute-start.7 = (bf16[256,128]{1,0:T(8,128)(2,1)S(1)}, bf16[256,128]{1,0:T(8,128)(2,1)S(1)}, u32[]{:S(2)}, u32[]{:S(2)}) collective-permute-start(bf16[256,128]{1,0:T(8,128)(2,1)S(1)} %get-tuple-element.55), channel_id=1, source_target_pairs={{0,16},{4,20},{8,24},{12,28},{1,17},{5,21},{9,25},{13,29},{2,18},{... | collective-permute-start | bytes 196616 | tf_op jit(solution)/shard_map/ppermute | solution.py:137
  40.0 4.7 %collective-permute-start.8 = (bf16[256,128]{1,0:T(8,128)(2,1)S(1)}, bf16[256,128]{1,0:T(8,128)(2,1)S(1)}, u32[]{:S(2)}, u32[]{:S(2)}) collective-permute-start(bf16[256,128]{1,0:T(8,128)(2,1)S(1)} %get-tuple-element.56), channel_id=1, source_target_pairs={{0,20},{4,16},{8,28},{12,24},{1,21},{5,17},{9,29},{13,25},{2,22},{... | collective-permute-start | bytes 196616 | tf_op jit(solution)/shard_map/ppermute | solution.py:137
  41.3 3.4 %collective-permute-start.9 = (bf16[256,128]{1,0:T(8,128)(2,1)S(1)}, bf16[256,128]{1,0:T(8,128)(2,1)S(1)}, u32[]{:S(2)}, u32[]{:S(2)}) collective-permute-start(bf16[256,128]{1,0:T(8,128)(2,1)S(1)} %get-tuple-element.57), channel_id=1, source_target_pairs={{0,24},{4,28},{8,16},{12,20},{1,25},{5,29},{9,17},{13,21},{2,26},{... | collective-permute-start | bytes 196616 | tf_op jit(solution)/shard_map/ppermute | solution.py:137
  45.7 23.0 %collective-permute-start.13 = (bf16[528,128]{1,0:T(8,128)(2,1)S(1)}, bf16[528,128]{1,0:T(8,128)(2,1)S(1)}, u32[]{:S(2)}, u32[]{:S(2)}) collective-permute-start(bf16[528,128]{1,0:T(8,128)(2,1)S(1)} %get-tuple-element.62), channel_id=1, source_target_pairs={{0,12},{4,8},{8,4},{12,0},{16,28},{20,24},{24,20},{28,16},{1,13},{... | collective-permute-start | bytes 405512 | tf_op jit(solution)/shard_map/ppermute | solution.py:137
  48.2 12.5 %collective-permute-start.17 = (bf16[272,128]{1,0:T(8,128)(2,1)S(1)}, bf16[272,128]{1,0:T(8,128)(2,1)S(1)}, u32[]{:S(2)}, u32[]{:S(2)}) collective-permute-start(bf16[272,128]{1,0:T(8,128)(2,1)S(1)} %get-tuple-element.66), channel_id=1, source_target_pairs={{0,28},{4,24},{8,20},{12,16},{1,29},{5,25},{9,21},{13,17},{2,30},{... | collective-permute-start | bytes 208904 | tf_op jit(solution)/shard_map/ppermute | solution.py:137
  54.5 14.3 %slice-start = ((s8[8388608]{0:T(1024)(128)(4,1)}), s8[4194304]{0:T(1024)(128)(4,1)S(1)}, s32[]{:S(2)}) async-start(s8[8388608]{0:T(1024)(128)(4,1)} %bitcast.2), calls=%async_computation | async-start | bytes 8388608
  55.5 13.2 %collective-permute-start.12 = (bf16[528,128]{1,0:T(8,128)(2,1)S(1)}, bf16[528,128]{1,0:T(8,128)(2,1)S(1)}, u32[]{:S(2)}, u32[]{:S(2)}) collective-permute-start(bf16[528,128]{1,0:T(8,128)(2,1)S(1)} %get-tuple-element.61), channel_id=1, source_target_pairs={{0,8},{4,12},{8,0},{12,4},{16,24},{20,28},{24,16},{28,20},{1,9},{5... | collective-permute-start | bytes 405512 | tf_op jit(solution)/shard_map/ppermute | solution.py:137
  55.6 6.4 %collective-permute-start.16 = (bf16[272,128]{1,0:T(8,128)(2,1)S(1)}, bf16[272,128]{1,0:T(8,128)(2,1)S(1)}, u32[]{:S(2)}, u32[]{:S(2)}) collective-permute-start(bf16[272,128]{1,0:T(8,128)(2,1)S(1)} %get-tuple-element.65), channel_id=1, source_target_pairs={{0,24},{4,28},{8,16},{12,20},{1,25},{5,29},{9,17},{13,21},{2,26},{... | collective-permute-start | bytes 208904 | tf_op jit(solution)/shard_map/ppermute | solution.py:137
  58.9 9.8 %collective-permute-start.11 = (bf16[528,128]{1,0:T(8,128)(2,1)S(1)}, bf16[528,128]{1,0:T(8,128)(2,1)S(1)}, u32[]{:S(2)}, u32[]{:S(2)}) collective-permute-start(bf16[528,128]{1,0:T(8,128)(2,1)S(1)} %get-tuple-element.60), channel_id=1, source_target_pairs={{0,4},{4,0},{8,12},{12,8},{16,20},{20,16},{24,28},{28,24},{1,5},{5... | collective-permute-start | bytes 405512 | tf_op jit(solution)/shard_map/ppermute | solution.py:137
  60.7 6.1 %collective-permute-start.15 = (bf16[272,128]{1,0:T(8,128)(2,1)S(1)}, bf16[272,128]{1,0:T(8,128)(2,1)S(1)}, u32[]{:S(2)}, u32[]{:S(2)}) collective-permute-start(bf16[272,128]{1,0:T(8,128)(2,1)S(1)} %get-tuple-element.64), channel_id=1, source_target_pairs={{0,20},{4,16},{8,28},{12,24},{1,21},{5,17},{9,29},{13,25},{2,22},{... | collective-permute-start | bytes 208904 | tf_op jit(solution)/shard_map/ppermute | solution.py:137
  62.0 6.7 %collective-permute-start.14 = (bf16[272,128]{1,0:T(8,128)(2,1)S(1)}, bf16[272,128]{1,0:T(8,128)(2,1)S(1)}, u32[]{:S(2)}, u32[]{:S(2)}) collective-permute-start(bf16[272,128]{1,0:T(8,128)(2,1)S(1)} %get-tuple-element.63), channel_id=1, source_target_pairs={{0,16},{4,20},{8,24},{12,28},{1,17},{5,21},{9,25},{13,29},{2,18},{... | collective-permute-start | bytes 208904 | tf_op jit(solution)/shard_map/ppermute | solution.py:137
  70.2 2.0 %collective-permute-start.18 = (bf16[256,1024]{1,0:T(8,128)(2,1)S(1)}, bf16[256,1024]{1,0:T(8,128)(2,1)S(1)}, u32[]{:S(2)}, u32[]{:S(2)}) collective-permute-start(bf16[256,1024]{1,0:T(8,128)(2,1)S(1)} %get-tuple-element.68), channel_id=1, source_target_pairs={{0,1},{1,0},{2,3},{3,2},{4,5},{5,4},{6,7},{7,6},{8,9},{9,8},{10,11... | collective-permute-start | bytes 1572872 | tf_op jit(solution)/shard_map/ppermute | solution.py:137
  73.6 3.0 %collective-permute-start.19 = (bf16[256,1024]{1,0:T(8,128)(2,1)S(1)}, bf16[256,1024]{1,0:T(8,128)(2,1)S(1)}, u32[]{:S(2)}, u32[]{:S(2)}) collective-permute-start(bf16[256,1024]{1,0:T(8,128)(2,1)S(1)} %shard_map.73), channel_id=1, source_target_pairs={{0,1},{1,0},{2,3},{3,2},{4,5},{5,4},{6,7},{7,6},{8,9},{9,8},{10,11... | collective-permute-start | bytes 1572872 | tf_op jit(solution)/shard_map/ppermute | solution.py:137
  73.8 14.2 %collective-permute-start.20 = (bf16[256,1024]{1,0:T(8,128)(2,1)S(1)}, bf16[256,1024]{1,0:T(8,128)(2,1)S(1)}, u32[]{:S(2)}, u32[]{:S(2)}) collective-permute-start(bf16[256,1024]{1,0:T(8,128)(2,1)S(1)} %add_convert_fusion.2), channel_id=1, source_target_pairs={{0,2},{1,3},{2,0},{3,1},{4,6},{5,7},{6,4},{7,5},{8,10},{9,11},{10,... | collective-permute-start | bytes 1572872 | tf_op jit(solution)/shard_map/ppermute | solution.py:137
  (1 other events, 13.2 us)

commit v2 on v1

--- a/solution.py
+++ b/solution.py
@@ -222,15 +222,16 @@
     return jnp.concatenate(rows, axis=0).astype(jnp.bfloat16)
 
 
-def unpack_stat(packed, size):
+def share_column(here, there, size):
     eye = square_eye(HEAD_DIM)
+    apart = there.astype(jnp.float32) - here.astype(jnp.float32)
     columns = []
-    packed = packed.astype(jnp.float32)
     for index in range(size // HEAD_DIM):
-        row = packed[3 * index : 3 * index + 1]
+        row = apart[3 * index : 3 * index + 1]
         for more in (1, 2):
-            row = row + packed[3 * index + more : 3 * index + more + 1]
-        columns.append(jnp.sum(jnp.where(eye, row, 0.0), axis=1, keepdims=True))
+            row = row + apart[3 * index + more : 3 * index + more + 1]
+        share = 1.0 / (1.0 + jnp.exp2(row))
+        columns.append(jnp.sum(jnp.where(eye, share, 0.0), axis=1, keepdims=True))
     return jnp.concatenate(columns, axis=0)
 
 
@@ -325,46 +326,53 @@
         peak_ref[flip] = peak
 
 
-def attend_across(half, flip, me_ref, *refs):
-    o_low, o_up, stat_ref, num_ref, total_ref, peak_ref = refs[:6]
-    weight_ref, far_total_ref, far_peak_ref = refs[6:9]
-    inner, cross_v = refs[9 : 9 + half], refs[9 + half : 9 + 2 * half]
-    across_ref, inner_ref, values = refs[9 + 2 * half :]
-    me = me_ref[0]
-    block = o_low.shape[1]
-    below = me < half
-    row_block = me % half ^ flip
-    inner_ref[:block] = o_low[row_block]
-    inner_ref[2 * block :] = stat_ref[row_block]
-
-    @pl.when(below)
+def attend_low(half, flips, me_ref, *refs):
+    weight_ref, total_ref, peak_ref = refs[:3]
+    inner, out_refs = refs[3 : 3 + half], refs[3 + half : -1]
+    values = refs[-1]
+    block = values.shape[0] // half
+
+    @pl.when(me_ref[0] < half)
     def _():
         for other in range(half):
             values[other * block : (other + 1) * block] = inner[other][2 * block : 3 * block]
-
-    @pl.when(jnp.logical_not(below))
+        for flip, out_ref in zip(flips, out_refs):
+            numerator = jnp.dot(weight_ref[flip], values[...], preferred_element_type=jnp.float32)
+            total = total_ref[flip]
+            out_ref[:block] = (numerator / total).astype(jnp.bfloat16)
+            out_ref[block:] = pack_stat(peak_ref[flip] * FACTOR + jnp.log2(total))
+
+
+def attend_up(half, flips, me_ref, *refs):
+    o_low, o_up, stat_ref, num_ref, total_ref, peak_ref = refs[:6]
+    weight_ref, far_total_ref, far_peak_ref = refs[6:9]
+    cross_v, out_refs, values = refs[9 : 9 + half], refs[9 + half : -1], refs[-1]
+    me = me_ref[0]
+    block = o_low.shape[1]
+    for flip, out_ref in zip(flips, out_refs):
+        row_block = me % half ^ flip
+        out_ref[:block] = o_low[row_block]
+        out_ref[2 * block :] = stat_ref[row_block]
+
+    @pl.when(me < half)
+    def _():
+        for flip, out_ref in zip(flips, out_refs):
+            out_ref[block : 2 * block] = o_up[me % half ^ flip]
+
+    @pl.when(me >= half)
     def _():
         for other in range(half):
             values[other * block : (other + 1) * block] = cross_v[other][...]
-
-    numerator = jnp.dot(weight_ref[flip], values[...], preferred_element_type=jnp.float32)
-    total, peak = far_total_ref[flip], far_peak_ref[flip]
-
-    @pl.when(below)
-    def _():
-        across_ref[:block] = (numerator / total).astype(jnp.bfloat16)
-        across_ref[block:] = pack_stat(peak * FACTOR + jnp.log2(total))
-        inner_ref[block : 2 * block] = o_up[row_block]
-
-    @pl.when(jnp.logical_not(below))
-    def _():
-        own_peak = peak_ref[row_block]
-        joint = jnp.maximum(peak, own_peak)
-        scale = jnp.exp2((peak - joint) * FACTOR)
-        own_scale = jnp.exp2((own_peak - joint) * FACTOR)
-        both = numerator * scale + num_ref[row_block] * own_scale
-        both_total = total * scale + total_ref[row_block] * own_scale
-        inner_ref[block : 2 * block] = (both / both_total).astype(jnp.bfloat16)
+        for flip, out_ref in zip(flips, out_refs):
+            row_block = me % half ^ flip
+            numerator = jnp.dot(weight_ref[flip], values[...], preferred_element_type=jnp.float32)
+            total, peak, own_peak = far_total_ref[flip], far_peak_ref[flip], peak_ref[row_block]
+            joint = jnp.maximum(peak, own_peak)
+            scale = jnp.exp2((peak - joint) * FACTOR)
+            own_scale = jnp.exp2((own_peak - joint) * FACTOR)
+            both = numerator * scale + num_ref[row_block] * own_scale
+            both_total = total * scale + total_ref[row_block] * own_scale
+            out_ref[block : 2 * block] = (both / both_total).astype(jnp.bfloat16)
 
 
 def join_heads(half, me_ref, inner, across, joined):
@@ -382,9 +390,7 @@
 
         @pl.when(me >= half)
         def _():
-            here = unpack_stat(inner[flip][2 * block :], block)
-            there = unpack_stat(across[flip][block:], block)
-            share = 1.0 / (1.0 + jnp.exp2(there - here))
+            share = share_column(inner[flip][2 * block :], across[flip][block:], block)
             mixed = inner[flip][:block].astype(jnp.float32) * share
             mixed = mixed + across[flip][:block].astype(jnp.float32) * (1.0 - share)
             joined[:, pl.ds(at, HEAD_DIM)] = mixed.astype(jnp.bfloat16)
@@ -426,7 +432,6 @@
         inner[flip] = swap(inner[flip], "seq", flip)
     for flip in down:
         cross[flip] = swap(cross[flip], "seq", half + flip)
-    for flip in down:
         cross_v[flip] = move(cross_v[flip], "seq", [(i, half + (i ^ flip)) for i in range(half)])
     w_held = held(out_weight)
     inner = [held(a) for a in inner]
@@ -449,21 +454,30 @@
         [pltpu.VMEM((half, block, HEAD_DIM), bf16)] * 2,
         flops=2 * 10**9,
     )(where, spans, full_ids, *inner, *cross)
-    state = [held(a) for a in (*own, *weights)]
+    weights = [held(a) for a in weights]
+    own = [held(a) for a in own]
     across, own_half = [None] * half, [None] * half
-    for flip in range(half):
-        far, near = own_kernel(
-            functools.partial(attend_across, half, flip),
-            [
-                shape((block + STAT_ROWS, HEAD_DIM), bf16),
-                shape((2 * block + STAT_ROWS, HEAD_DIM), bf16),
-            ],
-            [SMEM] + in_vmem(len(state) + 2 * half),
+    pairs = [(flip, flip - 1) for flip in range(half - 1, 0, -2)]
+    for flips in pairs:
+        lows = own_kernel(
+            functools.partial(attend_low, half, flips),
+            [shape((block + STAT_ROWS, HEAD_DIM), bf16)] * len(flips),
+            [SMEM] + in_vmem(3 + half),
             [pltpu.VMEM((half * block, HEAD_DIM), bf16)],
             flops=5 * 10**8,
-        )(where, *state, *inner, *cross_v)
-        across[flip] = move(far, "seq", [(i, half + (i ^ flip)) for i in range(half)])
-        own_half[flip] = swap(near, "seq", flip) if flip else near
+        )(where, *weights, *inner)
+        for flip, low in zip(flips, lows):
+            across[flip] = move(low, "seq", [(i, half + (i ^ flip)) for i in range(half)])
+    for flips in pairs:
+        ups = own_kernel(
+            functools.partial(attend_up, half, flips),
+            [shape((2 * block + STAT_ROWS, HEAD_DIM), bf16)] * len(flips),
+            [SMEM] + in_vmem(9 + half),
+            [pltpu.VMEM((half * block, HEAD_DIM), bf16)],
+            flops=5 * 10**8,
+        )(where, *own, *weights, *cross_v)
+        for flip, up in zip(flips, ups):
+            own_half[flip] = swap(up, "seq", flip) if flip else up
     came = [held(a) for a in own_half + across]
     width = out_weight.shape[1] // lax.axis_size("head")
     part = shape((block, width), bf16)

time: 89.7 us -> 86.1 us (0.960); the launches traced: 89.1 us -> 84.5 us
  starting transfers between devices: 48.1 us -> 34.2 us
  waiting for transfers between devices: 21.6 us -> 30.6 us
  local copies, waits for them, and re-layouts: 0.02 us -> 1.32 us
  Pallas kernels: 17.7 us -> 16.8 us
    ppermute x21, starting transfers between devices: 48.1 us -> 34.2 us  [move(): return lax.ppermute(block, axis, pairs)]
    ppermute x21, waiting for transfers between devices: 21.6 us -> 30.6 us  [move(): return lax.ppermute(block, axis, pairs)]
    unnamed x8, local copies, waits for them, and re-layouts: 0.02 us -> 1.32 us
  transfers between devices with their start and end apart: 21 -> 21, of which waited for: 6 -> 6; matrix products, arithmetic and copies ran while one was open for 0% -> 0% of each run, Pallas kernels for 13% -> 14%
where the time goes in v2:
time: 86.1 us; the launch traced here: 84.5 us
  starting transfers between devices  34.2 us (40%)
  waiting for transfers between devices  30.6 us (36%)
  Pallas kernels  16.8 us (20%)
  other arithmetic  1.33 us (2%)
  local copies, waits for them, and re-layouts  1.32 us (2%)
    ppermute x21, starting transfers between devices, move(): return lax.ppermute(block, axis, pairs)  34.2 us
    ppermute x21, waiting for transfers between devices, move(): return lax.ppermute(block, axis, pairs)  30.6 us
    pallas_call x1, Pallas kernels, half_path(): own_kernel(functools.partial(attend_own_half, half), [shape((half, block,...  4 us
    pallas_call x3, Pallas kernels, columns_of(): own_kernel(functools.partial(project, flip), [part], [SMEM] + in_vmem(2),...  3.76 us
    pallas_call x1, Pallas kernels, half_path(): own_kernel(functools.partial(deal, half), [shape((6 * block, HEAD_DIM), b...  2.45 us
    pallas_call x2, Pallas kernels, half_path(): own_kernel(functools.partial(attend_low, half, flips), [shape((block + ST...  2.04 us
    pallas_call x1, Pallas kernels, half_path(): own_kernel(functools.partial(weigh_across, half), [shape((half, block, ha...  2.01 us
  transfers between devices with their start and end apart: 21, of which 6 were waited for; matrix products, arithmetic and copies ran while one was open for 0% of the time, Pallas kernels for 14%

profile of v2, /device:TPU:0, one launch (start us, length us, event | category | flops | bytes accessed | tf_op | source)
XLA Modules:
  0.0 84.5 jit_solution(15741690240192846277)
XLA Ops:
  0.1 2.5 %shard_map.64 = (bf16[1536,128]{1,0:T(8,128)(2,1)S(1)}, bf16[1536,128]{1,0:T(8,128)(2,1)S(1)}, bf16[1536,128]{1,0:T(8,128)(2,1)S(1)}, bf16[1536,128]{1,0:T(8,128...) custom-call(s32[2]{0:T(128)S(1)} %pad_add_fusion.me_ref, ...), custom_call_target="tpu_custom_call" | custom-call | flops 100000000 | bytes 1000000 | tf_op jit(solution)/shard_map/pallas_call | solution.py:423
  2.5 3.1 %collective-permute-start = (bf16[1536,128]{1,0:T(8,128)(2,1)S(1)}, bf16[1536,128]{1,0:T(8,128)(2,1)S(1)}, u32[]{:S(2)}, u32[]{:S(2)}) collective-permute-start(bf16[1536,128]{1,0:T(8,128)(2,1)S(1)} %get-tuple-element.39), channel_id=1, source_target_pairs={{0,4},{4,0},{8,12},{12,8},{16,20},{20,16},{24,28},{28,24},{1,5},{5... | collective-permute-start | bytes 1179656 | tf_op jit(solution)/shard_map/ppermute | solution.py:137
  5.6 1.6 %collective-permute-start.1 = (bf16[1536,128]{1,0:T(8,128)(2,1)S(1)}, bf16[1536,128]{1,0:T(8,128)(2,1)S(1)}, u32[]{:S(2)}, u32[]{:S(2)}) collective-permute-start(bf16[1536,128]{1,0:T(8,128)(2,1)S(1)} %get-tuple-element.40), channel_id=1, source_target_pairs={{0,8},{4,12},{8,0},{12,4},{16,24},{20,28},{24,16},{28,20},{1,9},{5... | collective-permute-start | bytes 1179656 | tf_op jit(solution)/shard_map/ppermute | solution.py:137
  7.2 3.0 %collective-permute-start.3 = (bf16[256,128]{1,0:T(8,128)(2,1)S(1)}, bf16[256,128]{1,0:T(8,128)(2,1)S(1)}, u32[]{:S(2)}, u32[]{:S(2)}) collective-permute-start(bf16[256,128]{1,0:T(8,128)(2,1)S(1)} %get-tuple-element.48), channel_id=1, source_target_pairs={{0,16},{4,20},{8,24},{12,28},{16,0},{20,4},{24,8},{28,12},{1,17},{... | collective-permute-start | bytes 196616 | tf_op jit(solution)/shard_map/ppermute | solution.py:137
  10.2 1.3 %collective-permute-start.4 = (bf16[256,128]{1,0:T(8,128)(2,1)S(1)}, bf16[256,128]{1,0:T(8,128)(2,1)S(1)}, u32[]{:S(2)}, u32[]{:S(2)}) collective-permute-start(bf16[256,128]{1,0:T(8,128)(2,1)S(1)} %get-tuple-element.49), channel_id=1, source_target_pairs={{0,20},{4,16},{8,28},{12,24},{16,4},{20,0},{24,12},{28,8},{1,21},{... | collective-permute-start | bytes 196616 | tf_op jit(solution)/shard_map/ppermute | solution.py:137
  11.4 14.4 %collective-permute-done.3.refs_4_ = bf16[256,128]{1,0:T(8,128)(2,1)S(1)} collective-permute-done((bf16[256,128]{1,0:T(8,128)(2,1)S(1)}, bf16[256,128]{1,0:T(8,128)(2,1)S(1)}, u32[]{:S(2)}, u32[]{:S(2)}) %collective-permute-start.3) | collective-permute-done | bytes 65568 | tf_op jit(solution)/shard_map/ppermute | solution.py:137
  25.8 3.1 %collective-permute-start.5 = (bf16[256,128]{1,0:T(8,128)(2,1)S(1)}, bf16[256,128]{1,0:T(8,128)(2,1)S(1)}, u32[]{:S(2)}, u32[]{:S(2)}) collective-permute-start(bf16[256,128]{1,0:T(8,128)(2,1)S(1)} %get-tuple-element.50), channel_id=1, source_target_pairs={{0,24},{4,28},{8,16},{12,20},{16,8},{20,12},{24,0},{28,4},{1,25},{... | collective-permute-start | bytes 196616 | tf_op jit(solution)/shard_map/ppermute | solution.py:137
  29.7 2.2 %collective-permute-done.5.refs_6_ = bf16[256,128]{1,0:T(8,128)(2,1)S(1)} collective-permute-done((bf16[256,128]{1,0:T(8,128)(2,1)S(1)}, bf16[256,128]{1,0:T(8,128)(2,1)S(1)}, u32[]{:S(2)}, u32[]{:S(2)}) %collective-permute-start.5) | collective-permute-done | bytes 65568 | tf_op jit(solution)/shard_map/ppermute | solution.py:137
  31.9 5.0 %collective-permute-start.7 = (bf16[256,128]{1,0:T(8,128)(2,1)S(1)}, bf16[256,128]{1,0:T(8,128)(2,1)S(1)}, u32[]{:S(2)}, u32[]{:S(2)}) collective-permute-start(bf16[256,128]{1,0:T(8,128)(2,1)S(1)} %get-tuple-element.55), channel_id=1, source_target_pairs={{0,16},{4,20},{8,24},{12,28},{1,17},{5,21},{9,25},{13,29},{2,18},{... | collective-permute-start | bytes 196616 | tf_op jit(solution)/shard_map/ppermute | solution.py:137
  36.9 1.6 %collective-permute-start.8 = (bf16[256,128]{1,0:T(8,128)(2,1)S(1)}, bf16[256,128]{1,0:T(8,128)(2,1)S(1)}, u32[]{:S(2)}, u32[]{:S(2)}) collective-permute-start(bf16[256,128]{1,0:T(8,128)(2,1)S(1)} %get-tuple-element.56), channel_id=1, source_target_pairs={{0,20},{4,16},{8,28},{12,24},{1,21},{5,17},{9,29},{13,25},{2,22},{... | collective-permute-start | bytes 196616 | tf_op jit(solution)/shard_map/ppermute | solution.py:137
  38.5 1.4 %collective-permute-start.9 = (bf16[256,128]{1,0:T(8,128)(2,1)S(1)}, bf16[256,128]{1,0:T(8,128)(2,1)S(1)}, u32[]{:S(2)}, u32[]{:S(2)}) collective-permute-start(bf16[256,128]{1,0:T(8,128)(2,1)S(1)} %get-tuple-element.57), channel_id=1, source_target_pairs={{0,24},{4,28},{8,16},{12,20},{1,25},{5,29},{9,17},{13,21},{2,26},{... | collective-permute-start | bytes 196616 | tf_op jit(solution)/shard_map/ppermute | solution.py:137
  39.9 1.3 %collective-permute-start.10 = (bf16[256,128]{1,0:T(8,128)(2,1)S(1)}, bf16[256,128]{1,0:T(8,128)(2,1)S(1)}, u32[]{:S(2)}, u32[]{:S(2)}) collective-permute-start(bf16[256,128]{1,0:T(8,128)(2,1)S(1)} %get-tuple-element.58), channel_id=1, source_target_pairs={{0,28},{4,24},{8,20},{12,16},{1,29},{5,25},{9,21},{13,17},{2,30},{... | collective-permute-start | bytes 196616 | tf_op jit(solution)/shard_map/ppermute | solution.py:137
  42.5 2.0 %shard_map.66 = (bf16[4,256,1024]{2,1,0:T(8,128)(2,1)S(1)}, f32[4,256,1]{2,1,0:T(8,128)S(1)}, f32[4,256,1]{2,1,0:T(8,128)S(1)}) custom-call(s32[2]{0:T(128)S(1)} %pad_add_fusion.me_ref, s32[8]{0:T(128)S(1)} %copy-done, s32[2]{0:T(128)S(1)} %copy-done.1, bf16[1536,128]{1,0:T(8,128)(2,1)S(1)} %get-tuple-element.38.refs_0_.refs_3_, ...), custom_call_target="tpu_custom_call" | custom-call | flops 2000000000 | bytes 1000000 | tf_op jit(solution)/shard_map/pallas_call | solution.py:450
  45.6 1.3 %collective-permute-start.16 = (bf16[272,128]{1,0:T(8,128)(2,1)S(1)}, bf16[272,128]{1,0:T(8,128)(2,1)S(1)}, u32[]{:S(2)}, u32[]{:S(2)}) collective-permute-start(bf16[272,128]{1,0:T(8,128)(2,1)S(1)} %get-tuple-element.65), channel_id=1, source_target_pairs={{0,24},{4,28},{8,16},{12,20},{1,25},{5,29},{9,17},{13,21},{2,26},{... | collective-permute-start | bytes 208904 | tf_op jit(solution)/shard_map/ppermute | solution.py:137
  46.9 4.0 %shard_map.65 = (bf16[4,256,128]{2,1,0:T(8,128)(2,1)S(1)}, bf16[4,256,128]{2,1,0:T(8,128)(2,1)S(1)}, bf16[4,16,128]{2,1,0:T(8,128)(2,1)S(1)}, f32[4,256,128]{2,1...) custom-call(s32[2]{0:T(128)S(1)} %pad_add_fusion.me_ref, ...), custom_call_target="tpu_custom_call" | custom-call | flops 2000000000 | bytes 1000000 | tf_op jit(solution)/shard_map/pallas_call | solution.py:441
  50.9 1.6 %collective-permute-start.17 = (bf16[272,128]{1,0:T(8,128)(2,1)S(1)}, bf16[272,128]{1,0:T(8,128)(2,1)S(1)}, u32[]{:S(2)}, u32[]{:S(2)}) collective-permute-start(bf16[272,128]{1,0:T(8,128)(2,1)S(1)} %get-tuple-element.66), channel_id=1, source_target_pairs={{0,28},{4,24},{8,20},{12,16},{1,29},{5,25},{9,21},{13,17},{2,30},{... | collective-permute-start | bytes 208904 | tf_op jit(solution)/shard_map/ppermute | solution.py:137
  53.1 1.9 %collective-permute-start.12 = (bf16[528,128]{1,0:T(8,128)(2,1)S(1)}, bf16[528,128]{1,0:T(8,128)(2,1)S(1)}, u32[]{:S(2)}, u32[]{:S(2)}) collective-permute-start(bf16[528,128]{1,0:T(8,128)(2,1)S(1)} %get-tuple-element.61), channel_id=1, source_target_pairs={{0,8},{4,12},{8,0},{12,4},{16,24},{20,28},{24,16},{28,20},{1,9},{5... | collective-permute-start | bytes 405512 | tf_op jit(solution)/shard_map/ppermute | solution.py:137
  54.9 2.4 %collective-permute-start.13 = (bf16[528,128]{1,0:T(8,128)(2,1)S(1)}, bf16[528,128]{1,0:T(8,128)(2,1)S(1)}, u32[]{:S(2)}, u32[]{:S(2)}) collective-permute-start(bf16[528,128]{1,0:T(8,128)(2,1)S(1)} %get-tuple-element.62), channel_id=1, source_target_pairs={{0,12},{4,8},{8,4},{12,0},{16,28},{20,24},{24,20},{28,16},{1,13},{... | collective-permute-start | bytes 405512 | tf_op jit(solution)/shard_map/ppermute | solution.py:137
  59.0 1.9 %collective-permute-start.14 = (bf16[272,128]{1,0:T(8,128)(2,1)S(1)}, bf16[272,128]{1,0:T(8,128)(2,1)S(1)}, u32[]{:S(2)}, u32[]{:S(2)}) collective-permute-start(bf16[272,128]{1,0:T(8,128)(2,1)S(1)} %get-tuple-element.63), channel_id=1, source_target_pairs={{0,16},{4,20},{8,24},{12,28},{1,17},{5,21},{9,25},{13,29},{2,18},{... | collective-permute-start | bytes 208904 | tf_op jit(solution)/shard_map/ppermute | solution.py:137
  60.9 1.3 %collective-permute-start.15 = (bf16[272,128]{1,0:T(8,128)(2,1)S(1)}, bf16[272,128]{1,0:T(8,128)(2,1)S(1)}, u32[]{:S(2)}, u32[]{:S(2)}) collective-permute-start(bf16[272,128]{1,0:T(8,128)(2,1)S(1)} %get-tuple-element.64), channel_id=1, source_target_pairs={{0,20},{4,16},{8,28},{12,24},{1,21},{5,17},{9,29},{13,25},{2,22},{... | collective-permute-start | bytes 208904 | tf_op jit(solution)/shard_map/ppermute | solution.py:137
  62.8 1.3 %collective-permute-done.15.refs_5_ = bf16[272,128]{1,0:T(8,128)(2,1)S(1)} collective-permute-done((bf16[272,128]{1,0:T(8,128)(2,1)S(1)}, bf16[272,128]{1,0:T(8,128)(2,1)S(1)}, u32[]{:S(2)}, u32[]{:S(2)}) %collective-permute-start.15) | collective-permute-done | bytes 69664 | tf_op jit(solution)/shard_map/ppermute | solution.py:137
  64.2 1.4 %shard_map.71 = (bf16[256,1024]{1,0:T(8,128)(2,1)S(1)}, bf16[256,1024]{1,0:T(8,128)(2,1)S(1)}) custom-call(s32[2]{0:T(128)S(1)} %pad_add_fusion.me_ref, bf16[528,128]{1,0:T(8,128)(2,1)S(1)} %get-tuple-element.59.refs_0_, bf16[528,128]{1,0:T(8,128)(2,1)S(1)} %collective-permute-done.11.refs_1_, bf16[528,128]{1,0:T(8,128)(2,1)S(1)} %collective-permute-done.12.refs_2_, ...), custom_call_target="tpu_custom_call" | custom-call | flops 1000000000 | bytes 1000000 | tf_op jit(solution)/shard_map/pallas_call | solution.py:484
  69.2 1.5 %collective-permute-start.20 = (bf16[256,1024]{1,0:T(8,128)(2,1)S(1)}, bf16[256,1024]{1,0:T(8,128)(2,1)S(1)}, u32[]{:S(2)}, u32[]{:S(2)}) collective-permute-start(bf16[256,1024]{1,0:T(8,128)(2,1)S(1)} %add_convert_fusion.2), channel_id=1, source_target_pairs={{0,2},{1,3},{2,0},{3,1},{4,6},{5,7},{6,4},{7,5},{8,10},{9,11},{10,... | collective-permute-start | bytes 1572872 | tf_op jit(solution)/shard_map/ppermute | solution.py:137
  72.0 11.4 %collective-permute-done.20 = bf16[256,1024]{1,0:T(8,128)(2,1)S(1)} collective-permute-done((bf16[256,1024]{1,0:T(8,128)(2,1)S(1)}, bf16[256,1024]{1,0:T(8,128)(2,1)S(1)}, u32[]{:S(2)}, u32[]{:S(2)}) %collective-permute-start.20) | collective-permute-done | bytes 524320 | tf_op jit(solution)/shard_map/ppermute | solution.py:137
  (41 shorter events, 12.0 us)
Async XLA Ops:
  2.5 36.0 %collective-permute-start = (bf16[1536,128]{1,0:T(8,128)(2,1)S(1)}, bf16[1536,128]{1,0:T(8,128)(2,1)S(1)}, u32[]{:S(2)}, u32[]{:S(2)}) collective-permute-start(bf16[1536,128]{1,0:T(8,128)(2,1)S(1)} %get-tuple-element.39), channel_id=1, source_target_pairs={{0,4},{4,0},{8,12},{12,8},{16,20},{20,16},{24,28},{28,24},{1,5},{5... | collective-permute-start | bytes 1179656 | tf_op jit(solution)/shard_map/ppermute | solution.py:137
  5.6 34.3 %collective-permute-start.1 = (bf16[1536,128]{1,0:T(8,128)(2,1)S(1)}, bf16[1536,128]{1,0:T(8,128)(2,1)S(1)}, u32[]{:S(2)}, u32[]{:S(2)}) collective-permute-start(bf16[1536,128]{1,0:T(8,128)(2,1)S(1)} %get-tuple-element.40), channel_id=1, source_target_pairs={{0,8},{4,12},{8,0},{12,4},{16,24},{20,28},{24,16},{28,20},{1,9},{5... | collective-permute-start | bytes 1179656 | tf_op jit(solution)/shard_map/ppermute | solution.py:137
  7.2 34.0 %collective-permute-start.2 = (bf16[1536,128]{1,0:T(8,128)(2,1)S(1)}, bf16[1536,128]{1,0:T(8,128)(2,1)S(1)}, u32[]{:S(2)}, u32[]{:S(2)}) collective-permute-start(bf16[1536,128]{1,0:T(8,128)(2,1)S(1)} %get-tuple-element.41), channel_id=1, source_target_pairs={{0,12},{4,8},{8,4},{12,0},{16,28},{20,24},{24,20},{28,16},{1,13},{... | collective-permute-start | bytes 1179656 | tf_op jit(solution)/shard_map/ppermute | solution.py:137
  7.2 18.6 %collective-permute-start.3 = (bf16[256,128]{1,0:T(8,128)(2,1)S(1)}, bf16[256,128]{1,0:T(8,128)(2,1)S(1)}, u32[]{:S(2)}, u32[]{:S(2)}) collective-permute-start(bf16[256,128]{1,0:T(8,128)(2,1)S(1)} %get-tuple-element.48), channel_id=1, source_target_pairs={{0,16},{4,20},{8,24},{12,28},{16,0},{20,4},{24,8},{28,12},{1,17},{... | collective-permute-start | bytes 196616 | tf_op jit(solution)/shard_map/ppermute | solution.py:137
  10.2 18.7 %collective-permute-start.4 = (bf16[256,128]{1,0:T(8,128)(2,1)S(1)}, bf16[256,128]{1,0:T(8,128)(2,1)S(1)}, u32[]{:S(2)}, u32[]{:S(2)}) collective-permute-start(bf16[256,128]{1,0:T(8,128)(2,1)S(1)} %get-tuple-element.49), channel_id=1, source_target_pairs={{0,20},{4,16},{8,28},{12,24},{16,4},{20,0},{24,12},{28,8},{1,21},{... | collective-permute-start | bytes 196616 | tf_op jit(solution)/shard_map/ppermute | solution.py:137
  25.8 6.1 %collective-permute-start.5 = (bf16[256,128]{1,0:T(8,128)(2,1)S(1)}, bf16[256,128]{1,0:T(8,128)(2,1)S(1)}, u32[]{:S(2)}, u32[]{:S(2)}) collective-permute-start(bf16[256,128]{1,0:T(8,128)(2,1)S(1)} %get-tuple-element.50), channel_id=1, source_target_pairs={{0,24},{4,28},{8,16},{12,20},{16,8},{20,12},{24,0},{28,4},{1,25},{... | collective-permute-start | bytes 196616 | tf_op jit(solution)/shard_map/ppermute | solution.py:137
  28.9 8.0 %collective-permute-start.6 = (bf16[256,128]{1,0:T(8,128)(2,1)S(1)}, bf16[256,128]{1,0:T(8,128)(2,1)S(1)}, u32[]{:S(2)}, u32[]{:S(2)}) collective-permute-start(bf16[256,128]{1,0:T(8,128)(2,1)S(1)} %get-tuple-element.51), channel_id=1, source_target_pairs={{0,28},{4,24},{8,20},{12,16},{16,12},{20,8},{24,4},{28,0},{1,29},{... | collective-permute-start | bytes 196616 | tf_op jit(solution)/shard_map/ppermute | solution.py:137
  31.9 19.0 %collective-permute-start.7 = (bf16[256,128]{1,0:T(8,128)(2,1)S(1)}, bf16[256,128]{1,0:T(8,128)(2,1)S(1)}, u32[]{:S(2)}, u32[]{:S(2)}) collective-permute-start(bf16[256,128]{1,0:T(8,128)(2,1)S(1)} %get-tuple-element.55), channel_id=1, source_target_pairs={{0,16},{4,20},{8,24},{12,28},{1,17},{5,21},{9,25},{13,29},{2,18},{... | collective-permute-start | bytes 196616 | tf_op jit(solution)/shard_map/ppermute | solution.py:137
  36.9 15.5 %collective-permute-start.8 = (bf16[256,128]{1,0:T(8,128)(2,1)S(1)}, bf16[256,128]{1,0:T(8,128)(2,1)S(1)}, u32[]{:S(2)}, u32[]{:S(2)}) collective-permute-start(bf16[256,128]{1,0:T(8,128)(2,1)S(1)} %get-tuple-element.56), channel_id=1, source_target_pairs={{0,20},{4,16},{8,28},{12,24},{1,21},{5,17},{9,29},{13,25},{2,22},{... | collective-permute-start | bytes 196616 | tf_op jit(solution)/shard_map/ppermute | solution.py:137
  38.5 13.9 %collective-permute-start.9 = (bf16[256,128]{1,0:T(8,128)(2,1)S(1)}, bf16[256,128]{1,0:T(8,128)(2,1)S(1)}, u32[]{:S(2)}, u32[]{:S(2)}) collective-permute-start(bf16[256,128]{1,0:T(8,128)(2,1)S(1)} %get-tuple-element.57), channel_id=1, source_target_pairs={{0,24},{4,28},{8,16},{12,20},{1,25},{5,29},{9,17},{13,21},{2,26},{... | collective-permute-start | bytes 196616 | tf_op jit(solution)/shard_map/ppermute | solution.py:137
  39.9 12.6 %collective-permute-start.10 = (bf16[256,128]{1,0:T(8,128)(2,1)S(1)}, bf16[256,128]{1,0:T(8,128)(2,1)S(1)}, u32[]{:S(2)}, u32[]{:S(2)}) collective-permute-start(bf16[256,128]{1,0:T(8,128)(2,1)S(1)} %get-tuple-element.58), channel_id=1, source_target_pairs={{0,28},{4,24},{8,20},{12,16},{1,29},{5,25},{9,21},{13,17},{2,30},{... | collective-permute-start | bytes 196616 | tf_op jit(solution)/shard_map/ppermute | solution.py:137
  41.2 0.7 copy-start
  45.6 13.4 %collective-permute-start.16 = (bf16[272,128]{1,0:T(8,128)(2,1)S(1)}, bf16[272,128]{1,0:T(8,128)(2,1)S(1)}, u32[]{:S(2)}, u32[]{:S(2)}) collective-permute-start(bf16[272,128]{1,0:T(8,128)(2,1)S(1)} %get-tuple-element.65), channel_id=1, source_target_pairs={{0,24},{4,28},{8,16},{12,20},{1,25},{5,29},{9,17},{13,21},{2,26},{... | collective-permute-start | bytes 208904 | tf_op jit(solution)/shard_map/ppermute | solution.py:137
  50.9 13.3 %slice-start = ((s8[8388608]{0:T(1024)(128)(4,1)}), s8[4194304]{0:T(1024)(128)(4,1)S(1)}, s32[]{:S(2)}) async-start(s8[8388608]{0:T(1024)(128)(4,1)} %bitcast.2), calls=%async_computation | async-start | bytes 8388608
  50.9 10.0 %collective-permute-start.17 = (bf16[272,128]{1,0:T(8,128)(2,1)S(1)}, bf16[272,128]{1,0:T(8,128)(2,1)S(1)}, u32[]{:S(2)}, u32[]{:S(2)}) collective-permute-start(bf16[272,128]{1,0:T(8,128)(2,1)S(1)} %get-tuple-element.66), channel_id=1, source_target_pairs={{0,28},{4,24},{8,20},{12,16},{1,29},{5,25},{9,21},{13,17},{2,30},{... | collective-permute-start | bytes 208904 | tf_op jit(solution)/shard_map/ppermute | solution.py:137
  53.1 11.1 %collective-permute-start.12 = (bf16[528,128]{1,0:T(8,128)(2,1)S(1)}, bf16[528,128]{1,0:T(8,128)(2,1)S(1)}, u32[]{:S(2)}, u32[]{:S(2)}) collective-permute-start(bf16[528,128]{1,0:T(8,128)(2,1)S(1)} %get-tuple-element.61), channel_id=1, source_target_pairs={{0,8},{4,12},{8,0},{12,4},{16,24},{20,28},{24,16},{28,20},{1,9},{5... | collective-permute-start | bytes 405512 | tf_op jit(solution)/shard_map/ppermute | solution.py:137
  54.9 9.2 %slice-start.1 = ((s8[8388608]{0:T(1024)(128)(4,1)}), s8[4194304]{0:T(1024)(128)(4,1)S(1)}, s32[]{:S(2)}) async-start(s8[8388608]{0:T(1024)(128)(4,1)} %bitcast.2), calls=%async_computation.1 | async-start | bytes 8388608
  54.9 9.2 %collective-permute-start.13 = (bf16[528,128]{1,0:T(8,128)(2,1)S(1)}, bf16[528,128]{1,0:T(8,128)(2,1)S(1)}, u32[]{:S(2)}, u32[]{:S(2)}) collective-permute-start(bf16[528,128]{1,0:T(8,128)(2,1)S(1)} %get-tuple-element.62), channel_id=1, source_target_pairs={{0,12},{4,8},{8,4},{12,0},{16,28},{20,24},{24,20},{28,16},{1,13},{... | collective-permute-start | bytes 405512 | tf_op jit(solution)/shard_map/ppermute | solution.py:137
  57.9 6.3 %collective-permute-start.11 = (bf16[528,128]{1,0:T(8,128)(2,1)S(1)}, bf16[528,128]{1,0:T(8,128)(2,1)S(1)}, u32[]{:S(2)}, u32[]{:S(2)}) collective-permute-start(bf16[528,128]{1,0:T(8,128)(2,1)S(1)} %get-tuple-element.60), channel_id=1, source_target_pairs={{0,4},{4,0},{8,12},{12,8},{16,20},{20,16},{24,28},{28,24},{1,5},{5... | collective-permute-start | bytes 405512 | tf_op jit(solution)/shard_map/ppermute | solution.py:137
  59.0 3.8 %collective-permute-start.14 = (bf16[272,128]{1,0:T(8,128)(2,1)S(1)}, bf16[272,128]{1,0:T(8,128)(2,1)S(1)}, u32[]{:S(2)}, u32[]{:S(2)}) collective-permute-start(bf16[272,128]{1,0:T(8,128)(2,1)S(1)} %get-tuple-element.63), channel_id=1, source_target_pairs={{0,16},{4,20},{8,24},{12,28},{1,17},{5,21},{9,25},{13,29},{2,18},{... | collective-permute-start | bytes 208904 | tf_op jit(solution)/shard_map/ppermute | solution.py:137
  60.9 3.2 %collective-permute-start.15 = (bf16[272,128]{1,0:T(8,128)(2,1)S(1)}, bf16[272,128]{1,0:T(8,128)(2,1)S(1)}, u32[]{:S(2)}, u32[]{:S(2)}) collective-permute-start(bf16[272,128]{1,0:T(8,128)(2,1)S(1)} %get-tuple-element.64), channel_id=1, source_target_pairs={{0,20},{4,16},{8,28},{12,24},{1,21},{5,17},{9,29},{13,25},{2,22},{... | collective-permute-start | bytes 208904 | tf_op jit(solution)/shard_map/ppermute | solution.py:137
  65.6 2.0 %collective-permute-start.18 = (bf16[256,1024]{1,0:T(8,128)(2,1)S(1)}, bf16[256,1024]{1,0:T(8,128)(2,1)S(1)}, u32[]{:S(2)}, u32[]{:S(2)}) collective-permute-start(bf16[256,1024]{1,0:T(8,128)(2,1)S(1)} %get-tuple-element.68), channel_id=1, source_target_pairs={{0,1},{1,0},{2,3},{3,2},{4,5},{5,4},{6,7},{7,6},{8,9},{9,8},{10,11... | collective-permute-start | bytes 1572872 | tf_op jit(solution)/shard_map/ppermute | solution.py:137
  69.0 3.0 %collective-permute-start.19 = (bf16[256,1024]{1,0:T(8,128)(2,1)S(1)}, bf16[256,1024]{1,0:T(8,128)(2,1)S(1)}, u32[]{:S(2)}, u32[]{:S(2)}) collective-permute-start(bf16[256,1024]{1,0:T(8,128)(2,1)S(1)} %shard_map.73), channel_id=1, source_target_pairs={{0,1},{1,0},{2,3},{3,2},{4,5},{5,4},{6,7},{7,6},{8,9},{9,8},{10,11... | collective-permute-start | bytes 1572872 | tf_op jit(solution)/shard_map/ppermute | solution.py:137
  69.2 14.2 %collective-permute-start.20 = (bf16[256,1024]{1,0:T(8,128)(2,1)S(1)}, bf16[256,1024]{1,0:T(8,128)(2,1)S(1)}, u32[]{:S(2)}, u32[]{:S(2)}) collective-permute-start(bf16[256,1024]{1,0:T(8,128)(2,1)S(1)} %add_convert_fusion.2), channel_id=1, source_target_pairs={{0,2},{1,3},{2,0},{3,1},{4,6},{5,7},{6,4},{7,5},{8,10},{9,11},{10,... | collective-permute-start | bytes 1572872 | tf_op jit(solution)/shard_map/ppermute | solution.py:137
  (1 other events, 0.7 us)

commit v3 on v2

--- a/solution.py
+++ b/solution.py
@@ -166,9 +166,8 @@
     )
 
 
-def deal(half, me_ref, q_ref, k_ref, v_ref, *refs):
-    inner, cross, cross_v = refs[:half], refs[half : 2 * half], refs[2 * half : 3 * half]
-    sems = refs[3 * half]
+def deal(half, upper, me_ref, q_ref, k_ref, v_ref, *refs):
+    inner, cross, sems = refs[:half], refs[half : 2 * half], refs[2 * half]
     me = me_ref[0]
     low = me % half
     rows = q_ref.shape[0]
@@ -183,21 +182,20 @@
         )
 
     for flip in range(half - 1, -1, -1):
-        target = low ^ flip
-        for place in range(6):
-            source = (q_ref, k_ref, v_ref)[place % 3]
-            copy = fetch(source, target + place // 3 * half, inner[flip], place)
+        for place, source in enumerate((q_ref, k_ref, v_ref)):
+            copy = fetch(source, (low ^ flip) + upper * half, inner[flip], place)
             copy.start()
             waits.append(copy)
     for flip in range(half - 1, -1, -1):
         target = low ^ flip
-        below = fetch(k_ref, target + half, cross[flip], 0)
-        above = fetch(q_ref, target, cross[flip], 0)
-        pl.when(me < half)(below.start)
-        pl.when(me >= half)(above.start)
-        waits.append(above)
-        copy = fetch(v_ref, target + half, cross_v[flip], 0)
-        copy.start()
+        if upper:
+            copy = fetch(v_ref, target + half, cross[flip], 0)
+            copy.start()
+        else:
+            below = fetch(k_ref, target + half, cross[flip], 0)
+            copy = fetch(q_ref, target, cross[flip], 0)
+            pl.when(me < half)(below.start)
+            pl.when(me >= half)(copy.start)
         waits.append(copy)
     for copy in waits:
         copy.wait()
@@ -254,76 +252,65 @@
     )
 
 
-def attend_own_half(half, me_ref, *refs):
-    inner, (o_low, o_up, stat_ref, num_ref, total_ref, peak_ref, qkv) = refs[:half], refs[half:]
+def attend_own_half(half, upper, me_ref, *refs):
+    inner, (out_ref, *state_refs, qkv) = refs[:half], refs[half:]
     low = me_ref[0] % half
-    block = o_low.shape[1]
+    block = out_ref.shape[1]
     for flip in range(half):
         at = pl.multiple_of((low ^ flip) * block, block)
-        for place in range(6):
+        for place in range(3):
             qkv[place, pl.ds(at, block)] = inner[flip][place * block : (place + 1) * block]
     row = lax.broadcasted_iota(jnp.int32, (block, block), 0)
     causal = row >= lax.broadcasted_iota(jnp.int32, (block, block), 1)
-    for head in range(2):
-        for i in range(half):
-            q_tile = qkv[3 * head, i * block : (i + 1) * block]
-            pieces, value_tiles = [], []
-            for j in range(i + 1):
-                scores = score_tile(q_tile, qkv[3 * head + 1, j * block : (j + 1) * block])
-                pieces.append(jnp.where(causal, scores, NEG_FILL) if i == j else scores)
-                value_tiles.append(qkv[3 * head + 2, j * block : (j + 1) * block])
-            numerator, total, peak = softmax_rows(pieces, value_tiles)
-            result = (numerator / total).astype(jnp.bfloat16)
-            if head == 0:
-                o_low[i] = result
-                stat_ref[i] = pack_stat(peak * FACTOR + jnp.log2(total))
-            else:
-                o_up[i] = result
-                num_ref[i] = numerator
-                total_ref[i] = total
-                peak_ref[i] = peak
-
-
-def weigh_across(half, me_ref, spans_ref, full_ref, *refs):
+    for i in range(half):
+        q_tile = qkv[0, i * block : (i + 1) * block]
+        pieces, value_tiles = [], []
+        for j in range(i + 1):
+            scores = score_tile(q_tile, qkv[1, j * block : (j + 1) * block])
+            pieces.append(jnp.where(causal, scores, NEG_FILL) if i == j else scores)
+            value_tiles.append(qkv[2, j * block : (j + 1) * block])
+        numerator, total, peak = softmax_rows(pieces, value_tiles)
+        out_ref[i] = (numerator / total).astype(jnp.bfloat16)
+        if upper:
+            for state_ref, value in zip(state_refs, (numerator, total, peak)):
+                state_ref[i] = value
+        else:
+            state_refs[0][i] = pack_stat(peak * FACTOR + jnp.log2(total))
+
+
+def weigh_across(half, upper, me_ref, spans_ref, full_ref, *refs):
     inner, cross = refs[:half], refs[half : 2 * half]
-    weight_ref, total_ref, peak_ref, q_tiles, k_tiles = refs[2 * half :]
+    weight_ref, total_ref, peak_ref = refs[2 * half :]
     me, head = me_ref[0], me_ref[1]
     low = me % half
-    block = q_tiles.shape[1]
-    below = me < half
-
-    @pl.when(below)
+    block = cross[0].shape[0]
+
+    @pl.when(me >= half if upper else me < half)
     def _():
-        for other in range(half):
-            q_tiles[other] = cross[other][...]
-            k_tiles[other] = inner[other][block : 2 * block]
-
-    @pl.when(jnp.logical_not(below))
-    def _():
-        for other in range(half):
-            q_tiles[other] = inner[other][3 * block : 4 * block]
-            k_tiles[other] = cross[other][...]
-
-    local = jnp.where(below, low, low + half)
-    reach = spans_ref[local]
-    for place in range(full_ref.shape[0]):
-        reach = jnp.where(full_ref[place] == head * 2 * half + local, 2 * half * block, reach)
-    row = lax.broadcasted_iota(jnp.int32, (block, block), 0)
-    gap = row - lax.broadcasted_iota(jnp.int32, (block, block), 1)
-    for flip in range(half):
-        pieces = []
-        for other in range(half):
-            offset = (half + (low ^ flip) - (low ^ other)) * block
-            scores = score_tile(q_tiles[flip], k_tiles[other])
-            pieces.append(jnp.where(gap < reach - offset, scores, NEG_FILL))
-        peak = jnp.max(functools.reduce(jnp.maximum, pieces), axis=1, keepdims=True)
-        total = None
-        for other in range(half):
-            weights = jnp.exp2((pieces[other] - peak) * FACTOR)
-            weight_ref[flip, :, other * block : (other + 1) * block] = weights.astype(jnp.bfloat16)
-            total = weights if total is None else total + weights
-        total_ref[flip] = jnp.sum(total, axis=1, keepdims=True)
-        peak_ref[flip] = peak
+        local = low + upper * half
+        reach = spans_ref[local]
+        for place in range(full_ref.shape[0]):
+            reach = jnp.where(full_ref[place] == head * 2 * half + local, 2 * half * block, reach)
+        row = lax.broadcasted_iota(jnp.int32, (block, block), 0)
+        gap = row - lax.broadcasted_iota(jnp.int32, (block, block), 1)
+        for flip in range(half):
+            q_tile = inner[flip][:block] if upper else cross[flip][...]
+            pieces = []
+            for other in range(half):
+                k_tile = cross[other][...] if upper else inner[other][block : 2 * block]
+                offset = (half + (low ^ flip) - (low ^ other)) * block
+                scores = score_tile(q_tile, k_tile)
+                pieces.append(jnp.where(gap < reach - offset, scores, NEG_FILL))
+            peak = jnp.max(functools.reduce(jnp.maximum, pieces), axis=1, keepdims=True)
+            total = None
+            for other in range(half):
+                weights = jnp.exp2((pieces[other] - peak) * FACTOR)
+                weight_ref[flip, :, other * block : (other + 1) * block] = weights.astype(
+                    jnp.bfloat16
+                )
+                total = weights if total is None else total + weights
+            total_ref[flip] = jnp.sum(total, axis=1, keepdims=True)
+            peak_ref[flip] = peak
 
 
 def attend_low(half, flips, me_ref, *refs):
@@ -344,7 +331,7 @@
 
 
 def attend_up(half, flips, me_ref, *refs):
-    o_low, o_up, stat_ref, num_ref, total_ref, peak_ref = refs[:6]
+    o_low, stat_ref, o_up, num_ref, total_ref, peak_ref = refs[:6]
     weight_ref, far_total_ref, far_peak_ref = refs[6:9]
     cross_v, out_refs, values = refs[9 : 9 + half], refs[9 + half : -1], refs[-1]
     me = me_ref[0]
@@ -420,42 +407,48 @@
     down = range(half - 1, -1, -1)
     piece = shape((block, HEAD_DIM), bf16)
 
-    dealt = own_kernel(
-        functools.partial(deal, half),
-        [shape((6 * block, HEAD_DIM), bf16)] * half + [piece] * (2 * half),
-        [SMEM] + [pl.BlockSpec(memory_space=pltpu.HBM)] * 3,
-        [pltpu.SemaphoreType.DMA((8 * half,))],
-    )(where, *[pltpu.with_memory_space_constraint(a, pltpu.HBM) for a in (queries, keys_in, values_in)])
-    inner, cross, cross_v = dealt[:half], dealt[half : 2 * half], dealt[2 * half :]
-    inner, cross, cross_v = list(inner), list(cross), list(cross_v)
-    for flip in range(half - 1, 0, -1):
-        inner[flip] = swap(inner[flip], "seq", flip)
-    for flip in down:
-        cross[flip] = swap(cross[flip], "seq", half + flip)
-        cross_v[flip] = move(cross_v[flip], "seq", [(i, half + (i ^ flip)) for i in range(half)])
+    hbm = pl.BlockSpec(memory_space=pltpu.HBM)
+    ours = [pltpu.with_memory_space_constraint(a, pltpu.HBM) for a in (queries, keys_in, values_in)]
+    inner, cross = [], []
+    for upper in range(2):
+        dealt = own_kernel(
+            functools.partial(deal, half, upper),
+            [shape((3 * block, HEAD_DIM), bf16)] * half + [piece] * half,
+            [SMEM] + [hbm] * 3,
+            [pltpu.SemaphoreType.DMA((4 * half,))],
+        )(where, *ours)
+        inner.append(list(dealt[:half]))
+        cross.append(list(dealt[half:]))
+        for flip in range(half - 1, 0, -1):
+            inner[upper][flip] = swap(inner[upper][flip], "seq", flip)
+        for flip in down:
+            pairs = [(i, i ^ half ^ flip) for i in range(half if upper else n_seq)]
+            cross[upper][flip] = move(cross[upper][flip], "seq", pairs)
     w_held = held(out_weight)
-    inner = [held(a) for a in inner]
-    cross = [held(a) for a in cross]
-    cross_v = [held(a) for a in cross_v]
-
-    own = own_kernel(
-        functools.partial(attend_own_half, half),
-        [shape((half, block, HEAD_DIM), bf16)] * 2
-        + [shape((half, STAT_ROWS, HEAD_DIM), bf16), shape((half, block, HEAD_DIM), f32)]
-        + [shape((half, block, 1), f32)] * 2,
-        [SMEM] + in_vmem(half),
-        [pltpu.VMEM((6, half * block, HEAD_DIM), bf16)],
-        flops=2 * 10**9,
-    )(where, *inner)
-    weights = own_kernel(
-        functools.partial(weigh_across, half),
-        [shape((half, block, half * block), bf16)] + [shape((half, block, 1), f32)] * 2,
-        [SMEM] * 3 + in_vmem(2 * half),
-        [pltpu.VMEM((half, block, HEAD_DIM), bf16)] * 2,
-        flops=2 * 10**9,
-    )(where, spans, full_ids, *inner, *cross)
-    weights = [held(a) for a in weights]
-    own = [held(a) for a in own]
+    inner = [[held(a) for a in arrays] for arrays in inner]
+    cross_qk, cross_v = [[held(a) for a in arrays] for arrays in cross]
+
+    column = shape((half, block, 1), f32)
+    own, weights = [], []
+    for upper in range(2):
+        states = [shape((half, STAT_ROWS, HEAD_DIM), bf16)]
+        if upper:
+            states = [shape((half, block, HEAD_DIM), f32), column, column]
+        parts = own_kernel(
+            functools.partial(attend_own_half, half, upper),
+            [shape((half, block, HEAD_DIM), bf16)] + states,
+            [SMEM] + in_vmem(half),
+            [pltpu.VMEM((3, half * block, HEAD_DIM), bf16)],
+            flops=10**9,
+        )(where, *inner[upper])
+        own += [held(a) for a in parts]
+        parts = own_kernel(
+            functools.partial(weigh_across, half, upper),
+            [shape((half, block, half * block), bf16), column, column],
+            [SMEM] * 3 + in_vmem(2 * half),
+            flops=10**9,
+        )(where, spans, full_ids, *inner[upper], *cross_qk)
+        weights.append([held(a) for a in parts])
     across, own_half = [None] * half, [None] * half
     pairs = [(flip, flip - 1) for flip in range(half - 1, 0, -2)]
     for flips in pairs:
@@ -465,7 +458,7 @@
             [SMEM] + in_vmem(3 + half),
             [pltpu.VMEM((half * block, HEAD_DIM), bf16)],
             flops=5 * 10**8,
-        )(where, *weights, *inner)
+        )(where, *weights[0], *inner[0])
         for flip, low in zip(flips, lows):
             across[flip] = move(low, "seq", [(i, half + (i ^ flip)) for i in range(half)])
     for flips in pairs:
@@ -475,7 +468,7 @@
             [SMEM] + in_vmem(9 + half),
             [pltpu.VMEM((half * block, HEAD_DIM), bf16)],
             flops=5 * 10**8,
-        )(where, *own, *weights, *cross_v)
+        )(where, *own, *weights[1], *cross_v)
         for flip, up in zip(flips, ups):
             own_half[flip] = swap(up, "seq", flip) if flip else up
     came = [held(a) for a in own_half + across]

time: 86.1 us -> 83.9 us (0.974); the launches traced: 84.5 us -> 83.3 us
  waiting for transfers between devices: 30.6 us -> 23.1 us
  starting transfers between devices: 34.2 us -> 38.9 us
  Pallas kernels: 16.8 us -> 19.6 us
  local copies, waits for them, and re-layouts: 1.32 us -> 0.02 us
    ppermute x21 -> x24, waiting for transfers between devices: 30.6 us -> 23.1 us  [move(): return lax.ppermute(block, axis, pairs)]
    ppermute x21 -> x24, starting transfers between devices: 34.2 us -> 38.9 us  [move(): return lax.ppermute(block, axis, pairs)]
    pallas_call x3 -> x6, Pallas kernels: 8.46 us -> 11.1 us  [the longest x2 4.63 us: half_path(): own_kernel(functools.partial(attend_own_half, half, upper), [shape((half,...]
    unnamed x8, local copies, waits for them, and re-layouts: 1.32 us -> 0.02 us
  transfers between devices with their start and end apart: 21 -> 24, of which waited for: 6 -> 6; matrix products, arithmetic and copies ran while one was open for 0% -> 0% of each run, Pallas kernels for 14% -> 18%
where the time goes in v3:
time: 83.9 us; the launch traced here: 83.3 us
  starting transfers between devices  38.9 us (46%)
  waiting for transfers between devices  23.1 us (28%)
  Pallas kernels  19.6 us (23%)
  other arithmetic  1.33 us (2%)
    ppermute x24, starting transfers between devices, move(): return lax.ppermute(block, axis, pairs)  38.9 us
    ppermute x24, waiting for transfers between devices, move(): return lax.ppermute(block, axis, pairs)  23.1 us
    pallas_call x2, Pallas kernels, half_path(): own_kernel(functools.partial(attend_own_half, half, upper), [shape((half,...  4.63 us
    pallas_call x2, Pallas kernels, half_path(): own_kernel(functools.partial(deal, half, upper), [shape((3 * block, HEAD_...  3.91 us
    pallas_call x3, Pallas kernels, columns_of(): own_kernel(functools.partial(project, flip), [part], [SMEM] + in_vmem(2),...  3.76 us
    pallas_call x2, Pallas kernels, half_path(): own_kernel(functools.partial(weigh_across, half, upper), [shape((half, bl...  2.56 us
    pallas_call x2, Pallas kernels, half_path(): own_kernel(functools.partial(attend_low, half, flips), [shape((block + ST...  2.03 us
  transfers between devices with their start and end apart: 24, of which 6 were waited for; matrix products, arithmetic and copies ran while one was open for 0% of the time, Pallas kernels for 18%

profile of v3, /device:TPU:0, one launch (start us, length us, event | category | flops | bytes accessed | tf_op | source)
XLA Modules:
  0.0 83.3 jit_solution(5205771474685972045)
XLA Ops:
  0.1 2.0 %shard_map.64 = (bf16[768,128]{1,0:T(8,128)(2,1)S(1)}, bf16[768,128]{1,0:T(8,128)(2,1)S(1)}, bf16[768,128]{1,0:T(8,128)(2,1)S(1)}, bf16[768,128]{1,0:T(8,128)(2,...) custom-call(s32[2]{0:T(128)S(1)} %pad_add_fusion.me_ref, ...), custom_call_target="tpu_custom_call" | custom-call | flops 100000000 | bytes 1000000 | tf_op jit(solution)/shard_map/pallas_call | solution.py:414
  2.0 3.1 %collective-permute-start = (bf16[768,128]{1,0:T(8,128)(2,1)S(1)}, bf16[768,128]{1,0:T(8,128)(2,1)S(1)}, u32[]{:S(2)}, u32[]{:S(2)}) collective-permute-start(bf16[768,128]{1,0:T(8,128)(2,1)S(1)} %get-tuple-element.46), channel_id=1, source_target_pairs={{0,4},{4,0},{8,12},{12,8},{16,20},{20,16},{24,28},{28,24},{1,5},{5... | collective-permute-start | bytes 589832 | tf_op jit(solution)/shard_map/ppermute | solution.py:137
  5.1 1.6 %collective-permute-start.1 = (bf16[768,128]{1,0:T(8,128)(2,1)S(1)}, bf16[768,128]{1,0:T(8,128)(2,1)S(1)}, u32[]{:S(2)}, u32[]{:S(2)}) collective-permute-start(bf16[768,128]{1,0:T(8,128)(2,1)S(1)} %get-tuple-element.47), channel_id=1, source_target_pairs={{0,8},{4,12},{8,0},{12,4},{16,24},{20,28},{24,16},{28,20},{1,9},{5... | collective-permute-start | bytes 589832 | tf_op jit(solution)/shard_map/ppermute | solution.py:137
  6.7 3.0 %collective-permute-start.6 = (bf16[256,128]{1,0:T(8,128)(2,1)S(1)}, bf16[256,128]{1,0:T(8,128)(2,1)S(1)}, u32[]{:S(2)}, u32[]{:S(2)}) collective-permute-start(bf16[256,128]{1,0:T(8,128)(2,1)S(1)} %get-tuple-element.59), channel_id=1, source_target_pairs={{0,16},{4,20},{8,24},{12,28},{16,0},{20,4},{24,8},{28,12},{1,17},{... | collective-permute-start | bytes 196616 | tf_op jit(solution)/shard_map/ppermute | solution.py:137
  11.0 5.9 %collective-permute-done.6.refs_4_ = bf16[256,128]{1,0:T(8,128)(2,1)S(1)} collective-permute-done((bf16[256,128]{1,0:T(8,128)(2,1)S(1)}, bf16[256,128]{1,0:T(8,128)(2,1)S(1)}, u32[]{:S(2)}, u32[]{:S(2)}) %collective-permute-start.6) | collective-permute-done | bytes 65568 | tf_op jit(solution)/shard_map/ppermute | solution.py:137
  16.9 3.0 %collective-permute-start.8 = (bf16[256,128]{1,0:T(8,128)(2,1)S(1)}, bf16[256,128]{1,0:T(8,128)(2,1)S(1)}, u32[]{:S(2)}, u32[]{:S(2)}) collective-permute-start(bf16[256,128]{1,0:T(8,128)(2,1)S(1)} %get-tuple-element.61), channel_id=1, source_target_pairs={{0,24},{4,28},{8,16},{12,20},{16,8},{20,12},{24,0},{28,4},{1,25},{... | collective-permute-start | bytes 196616 | tf_op jit(solution)/shard_map/ppermute | solution.py:137
  20.7 2.0 %shard_map.66 = (bf16[768,128]{1,0:T(8,128)(2,1)S(1)}, bf16[768,128]{1,0:T(8,128)(2,1)S(1)}, bf16[768,128]{1,0:T(8,128)(2,1)S(1)}, bf16[768,128]{1,0:T(8,128)(2,...) custom-call(s32[2]{0:T(128)S(1)} %pad_add_fusion.me_ref, ...), custom_call_target="tpu_custom_call" | custom-call | flops 100000000 | bytes 1000000 | tf_op jit(solution)/shard_map/pallas_call | solution.py:414
  22.9 1.3 %collective-permute-start.3 = (bf16[768,128]{1,0:T(8,128)(2,1)S(1)}, bf16[768,128]{1,0:T(8,128)(2,1)S(1)}, u32[]{:S(2)}, u32[]{:S(2)}) collective-permute-start(bf16[768,128]{1,0:T(8,128)(2,1)S(1)} %get-tuple-element.52), channel_id=1, source_target_pairs={{0,4},{4,0},{8,12},{12,8},{16,20},{20,16},{24,28},{28,24},{1,5},{5... | collective-permute-start | bytes 589832 | tf_op jit(solution)/shard_map/ppermute | solution.py:137
  24.3 2.9 %collective-permute-done.9.refs_7_ = bf16[256,128]{1,0:T(8,128)(2,1)S(1)} collective-permute-done((bf16[256,128]{1,0:T(8,128)(2,1)S(1)}, bf16[256,128]{1,0:T(8,128)(2,1)S(1)}, u32[]{:S(2)}, u32[]{:S(2)}) %collective-permute-start.9) | collective-permute-done | bytes 65568 | tf_op jit(solution)/shard_map/ppermute | solution.py:137
  28.9 2.8 %collective-permute-start.10 = (bf16[256,128]{1,0:T(8,128)(2,1)S(1)}, bf16[256,128]{1,0:T(8,128)(2,1)S(1)}, u32[]{:S(2)}, u32[]{:S(2)}) collective-permute-start(bf16[256,128]{1,0:T(8,128)(2,1)S(1)} %get-tuple-element.66), channel_id=1, source_target_pairs={{0,16},{4,20},{8,24},{12,28},{1,17},{5,21},{9,25},{13,29},{2,18},{... | collective-permute-start | bytes 196616 | tf_op jit(solution)/shard_map/ppermute | solution.py:137
  31.7 2.1 %collective-permute-start.11 = (bf16[256,128]{1,0:T(8,128)(2,1)S(1)}, bf16[256,128]{1,0:T(8,128)(2,1)S(1)}, u32[]{:S(2)}, u32[]{:S(2)}) collective-permute-start(bf16[256,128]{1,0:T(8,128)(2,1)S(1)} %get-tuple-element.67), channel_id=1, source_target_pairs={{0,20},{4,16},{8,28},{12,24},{1,21},{5,17},{9,29},{13,25},{2,22},{... | collective-permute-start | bytes 196616 | tf_op jit(solution)/shard_map/ppermute | solution.py:137
  33.8 2.0 %shard_map.71 = (bf16[4,256,1024]{2,1,0:T(8,128)(2,1)S(1)}, f32[4,256,1]{2,1,0:T(8,128)S(1)}, f32[4,256,1]{2,1,0:T(8,128)S(1)}) custom-call(s32[2]{0:T(128)S(1)} %pad_add_fusion.me_ref, s32[8]{0:T(128)S(1)} %copy-done, s32[2]{0:T(128)S(1)} %copy-done.1, bf16[768,128]{1,0:T(8,128)(2,1)S(1)} %get-tuple-element.45.refs_0_.refs_3_, ...), custom_call_target="tpu_custom_call" | custom-call | flops 1000000000 | bytes 1000000 | tf_op jit(solution)/shard_map/pallas_call | solution.py:445
  36.8 2.3 %shard_map.65 = (bf16[4,256,128]{2,1,0:T(8,128)(2,1)S(1)}, bf16[4,16,128]{2,1,0:T(8,128)(2,1)S(1)}) custom-call(s32[2]{0:T(128)S(1)} %pad_add_fusion.me_ref, bf16[768,128]{1,0:T(8,128)(2,1)S(1)} %get-tuple-element.45.refs_0_.refs_3_, bf16[768,128]{1,0:T(8,128)(2,1)S(1)} %collective-permute-done.refs_1_.refs_4_, ...), custom_call_target="tpu_custom_call" | custom-call | flops 1000000000 | bytes 1000000 | tf_op jit(solution)/shard_map/pallas_call | solution.py:437
  39.2 1.3 %collective-permute-start.12 = (bf16[256,128]{1,0:T(8,128)(2,1)S(1)}, bf16[256,128]{1,0:T(8,128)(2,1)S(1)}, u32[]{:S(2)}, u32[]{:S(2)}) collective-permute-start(bf16[256,128]{1,0:T(8,128)(2,1)S(1)} %get-tuple-element.68), channel_id=1, source_target_pairs={{0,24},{4,28},{8,16},{12,20},{1,25},{5,29},{9,17},{13,21},{2,26},{... | collective-permute-start | bytes 196616 | tf_op jit(solution)/shard_map/ppermute | solution.py:137
  41.8 1.3 %collective-permute-start.19 = (bf16[272,128]{1,0:T(8,128)(2,1)S(1)}, bf16[272,128]{1,0:T(8,128)(2,1)S(1)}, u32[]{:S(2)}, u32[]{:S(2)}) collective-permute-start(bf16[272,128]{1,0:T(8,128)(2,1)S(1)} %get-tuple-element.79), channel_id=1, source_target_pairs={{0,24},{4,28},{8,16},{12,20},{1,25},{5,29},{9,17},{13,21},{2,26},{... | collective-permute-start | bytes 208904 | tf_op jit(solution)/shard_map/ppermute | solution.py:137
  43.7 2.3 %shard_map.67 = (bf16[4,256,128]{2,1,0:T(8,128)(2,1)S(1)}, f32[4,256,128]{2,1,0:T(8,128)S(1)}, f32[4,256,1]{2,1,0:T(8,128)S(1)}, f32[4,256,1]{2,1,0:T(8,128)S(1)}) custom-call(s32[2]{0:T(128)S(1)} %pad_add_fusion.me_ref, bf16[768,128]{1,0:T(8,128)(2,1)S(1)} %get-tuple-element.51.refs_0_, bf16[768,128]{1,0:T(8,128)(2,1)S(1)} %collective-permute-done.3.refs_1_, ...), custom_call_target="tpu_custom_call" | custom-call | flops 1000000000 | bytes 1000000 | tf_op jit(solution)/shard_map/pallas_call | solution.py:437
  46.0 1.3 %collective-permute-start.20 = (bf16[272,128]{1,0:T(8,128)(2,1)S(1)}, bf16[272,128]{1,0:T(8,128)(2,1)S(1)}, u32[]{:S(2)}, u32[]{:S(2)}) collective-permute-start(bf16[272,128]{1,0:T(8,128)(2,1)S(1)} %get-tuple-element.80), channel_id=1, source_target_pairs={{0,28},{4,24},{8,20},{12,16},{1,29},{5,25},{9,21},{13,17},{2,30},{... | collective-permute-start | bytes 208904 | tf_op jit(solution)/shard_map/ppermute | solution.py:137
  48.7 1.7 %collective-permute-start.16 = (bf16[528,128]{1,0:T(8,128)(2,1)S(1)}, bf16[528,128]{1,0:T(8,128)(2,1)S(1)}, u32[]{:S(2)}, u32[]{:S(2)}) collective-permute-start(bf16[528,128]{1,0:T(8,128)(2,1)S(1)} %get-tuple-element.73), channel_id=1, source_target_pairs={{0,12},{4,8},{8,4},{12,0},{16,28},{20,24},{24,20},{28,16},{1,13},{... | collective-permute-start | bytes 405512 | tf_op jit(solution)/shard_map/ppermute | solution.py:137
  53.1 5.1 %collective-permute-start.17 = (bf16[272,128]{1,0:T(8,128)(2,1)S(1)}, bf16[272,128]{1,0:T(8,128)(2,1)S(1)}, u32[]{:S(2)}, u32[]{:S(2)}) collective-permute-start(bf16[272,128]{1,0:T(8,128)(2,1)S(1)} %get-tuple-element.77), channel_id=1, source_target_pairs={{0,16},{4,20},{8,24},{12,28},{1,17},{5,21},{9,25},{13,29},{2,18},{... | collective-permute-start | bytes 208904 | tf_op jit(solution)/shard_map/ppermute | solution.py:137
  58.3 2.6 %collective-permute-start.18 = (bf16[272,128]{1,0:T(8,128)(2,1)S(1)}, bf16[272,128]{1,0:T(8,128)(2,1)S(1)}, u32[]{:S(2)}, u32[]{:S(2)}) collective-permute-start(bf16[272,128]{1,0:T(8,128)(2,1)S(1)} %get-tuple-element.78), channel_id=1, source_target_pairs={{0,20},{4,16},{8,28},{12,24},{1,21},{5,17},{9,29},{13,25},{2,22},{... | collective-permute-start | bytes 208904 | tf_op jit(solution)/shard_map/ppermute | solution.py:137
  60.9 1.9 %collective-permute-done.18.refs_5_ = bf16[272,128]{1,0:T(8,128)(2,1)S(1)} collective-permute-done((bf16[272,128]{1,0:T(8,128)(2,1)S(1)}, bf16[272,128]{1,0:T(8,128)(2,1)S(1)}, u32[]{:S(2)}, u32[]{:S(2)}) %collective-permute-start.18) | collective-permute-done | bytes 69664 | tf_op jit(solution)/shard_map/ppermute | solution.py:137
  62.8 1.6 %shard_map.74 = (bf16[256,1024]{1,0:T(8,128)(2,1)S(1)}, bf16[256,1024]{1,0:T(8,128)(2,1)S(1)}) custom-call(s32[2]{0:T(128)S(1)} %pad_add_fusion.me_ref, bf16[528,128]{1,0:T(8,128)(2,1)S(1)} %get-tuple-element.70.refs_0_, bf16[528,128]{1,0:T(8,128)(2,1)S(1)} %collective-permute-done.14.refs_1_, bf16[528,128]{1,0:T(8,128)(2,1)S(1)} %collective-permute-done.15.refs_2_, ...), custom_call_target="tpu_custom_call" | custom-call | flops 1000000000 | bytes 1000000 | tf_op jit(solution)/shard_map/pallas_call | solution.py:477
  68.1 1.5 %collective-permute-start.23 = (bf16[256,1024]{1,0:T(8,128)(2,1)S(1)}, bf16[256,1024]{1,0:T(8,128)(2,1)S(1)}, u32[]{:S(2)}, u32[]{:S(2)}) collective-permute-start(bf16[256,1024]{1,0:T(8,128)(2,1)S(1)} %add_convert_fusion.2), channel_id=1, source_target_pairs={{0,2},{1,3},{2,0},{3,1},{4,6},{5,7},{6,4},{7,5},{8,10},{9,11},{10,... | collective-permute-start | bytes 1572872 | tf_op jit(solution)/shard_map/ppermute | solution.py:137
  70.8 11.5 %collective-permute-done.23 = bf16[256,1024]{1,0:T(8,128)(2,1)S(1)} collective-permute-done((bf16[256,1024]{1,0:T(8,128)(2,1)S(1)}, bf16[256,1024]{1,0:T(8,128)(2,1)S(1)}, u32[]{:S(2)}, u32[]{:S(2)}) %collective-permute-start.23) | collective-permute-done | bytes 524320 | tf_op jit(solution)/shard_map/ppermute | solution.py:137
  (50 shorter events, 17.1 us)
Async XLA Ops:
  2.0 25.7 %collective-permute-start = (bf16[768,128]{1,0:T(8,128)(2,1)S(1)}, bf16[768,128]{1,0:T(8,128)(2,1)S(1)}, u32[]{:S(2)}, u32[]{:S(2)}) collective-permute-start(bf16[768,128]{1,0:T(8,128)(2,1)S(1)} %get-tuple-element.46), channel_id=1, source_target_pairs={{0,4},{4,0},{8,12},{12,8},{16,20},{20,16},{24,28},{28,24},{1,5},{5... | collective-permute-start | bytes 589832 | tf_op jit(solution)/shard_map/ppermute | solution.py:137
  5.1 23.7 %collective-permute-start.1 = (bf16[768,128]{1,0:T(8,128)(2,1)S(1)}, bf16[768,128]{1,0:T(8,128)(2,1)S(1)}, u32[]{:S(2)}, u32[]{:S(2)}) collective-permute-start(bf16[768,128]{1,0:T(8,128)(2,1)S(1)} %get-tuple-element.47), channel_id=1, source_target_pairs={{0,8},{4,12},{8,0},{12,4},{16,24},{20,28},{24,16},{28,20},{1,9},{5... | collective-permute-start | bytes 589832 | tf_op jit(solution)/shard_map/ppermute | solution.py:137
  6.7 25.0 %collective-permute-start.2 = (bf16[768,128]{1,0:T(8,128)(2,1)S(1)}, bf16[768,128]{1,0:T(8,128)(2,1)S(1)}, u32[]{:S(2)}, u32[]{:S(2)}) collective-permute-start(bf16[768,128]{1,0:T(8,128)(2,1)S(1)} %get-tuple-element.48), channel_id=1, source_target_pairs={{0,12},{4,8},{8,4},{12,0},{16,28},{20,24},{24,20},{28,16},{1,13},{... | collective-permute-start | bytes 589832 | tf_op jit(solution)/shard_map/ppermute | solution.py:137
  6.7 10.2 %collective-permute-start.6 = (bf16[256,128]{1,0:T(8,128)(2,1)S(1)}, bf16[256,128]{1,0:T(8,128)(2,1)S(1)}, u32[]{:S(2)}, u32[]{:S(2)}) collective-permute-start(bf16[256,128]{1,0:T(8,128)(2,1)S(1)} %get-tuple-element.59), channel_id=1, source_target_pairs={{0,16},{4,20},{8,24},{12,28},{16,0},{20,4},{24,8},{28,12},{1,17},{... | collective-permute-start | bytes 196616 | tf_op jit(solution)/shard_map/ppermute | solution.py:137
  9.7 10.2 %collective-permute-start.7 = (bf16[256,128]{1,0:T(8,128)(2,1)S(1)}, bf16[256,128]{1,0:T(8,128)(2,1)S(1)}, u32[]{:S(2)}, u32[]{:S(2)}) collective-permute-start(bf16[256,128]{1,0:T(8,128)(2,1)S(1)} %get-tuple-element.60), channel_id=1, source_target_pairs={{0,20},{4,16},{8,28},{12,24},{16,4},{20,0},{24,12},{28,8},{1,21},{... | collective-permute-start | bytes 196616 | tf_op jit(solution)/shard_map/ppermute | solution.py:137
  16.9 6.1 %collective-permute-start.8 = (bf16[256,128]{1,0:T(8,128)(2,1)S(1)}, bf16[256,128]{1,0:T(8,128)(2,1)S(1)}, u32[]{:S(2)}, u32[]{:S(2)}) collective-permute-start(bf16[256,128]{1,0:T(8,128)(2,1)S(1)} %get-tuple-element.61), channel_id=1, source_target_pairs={{0,24},{4,28},{8,16},{12,20},{16,8},{20,12},{24,0},{28,4},{1,25},{... | collective-permute-start | bytes 196616 | tf_op jit(solution)/shard_map/ppermute | solution.py:137
  19.9 7.2 %collective-permute-start.9 = (bf16[256,128]{1,0:T(8,128)(2,1)S(1)}, bf16[256,128]{1,0:T(8,128)(2,1)S(1)}, u32[]{:S(2)}, u32[]{:S(2)}) collective-permute-start(bf16[256,128]{1,0:T(8,128)(2,1)S(1)} %get-tuple-element.62), channel_id=1, source_target_pairs={{0,28},{4,24},{8,20},{12,16},{16,12},{20,8},{24,4},{28,0},{1,29},{... | collective-permute-start | bytes 196616 | tf_op jit(solution)/shard_map/ppermute | solution.py:137
  22.9 16.2 %collective-permute-start.3 = (bf16[768,128]{1,0:T(8,128)(2,1)S(1)}, bf16[768,128]{1,0:T(8,128)(2,1)S(1)}, u32[]{:S(2)}, u32[]{:S(2)}) collective-permute-start(bf16[768,128]{1,0:T(8,128)(2,1)S(1)} %get-tuple-element.52), channel_id=1, source_target_pairs={{0,4},{4,0},{8,12},{12,8},{16,20},{20,16},{24,28},{28,24},{1,5},{5... | collective-permute-start | bytes 589832 | tf_op jit(solution)/shard_map/ppermute | solution.py:137
  27.1 13.4 %collective-permute-start.4 = (bf16[768,128]{1,0:T(8,128)(2,1)S(1)}, bf16[768,128]{1,0:T(8,128)(2,1)S(1)}, u32[]{:S(2)}, u32[]{:S(2)}) collective-permute-start(bf16[768,128]{1,0:T(8,128)(2,1)S(1)} %get-tuple-element.53), channel_id=1, source_target_pairs={{0,8},{4,12},{8,0},{12,4},{16,24},{20,28},{24,16},{28,20},{1,9},{5... | collective-permute-start | bytes 589832 | tf_op jit(solution)/shard_map/ppermute | solution.py:137
  27.8 14.0 %collective-permute-start.5 = (bf16[768,128]{1,0:T(8,128)(2,1)S(1)}, bf16[768,128]{1,0:T(8,128)(2,1)S(1)}, u32[]{:S(2)}, u32[]{:S(2)}) collective-permute-start(bf16[768,128]{1,0:T(8,128)(2,1)S(1)} %get-tuple-element.54), channel_id=1, source_target_pairs={{0,12},{4,8},{8,4},{12,0},{16,28},{20,24},{24,20},{28,16},{1,13},{... | collective-permute-start | bytes 589832 | tf_op jit(solution)/shard_map/ppermute | solution.py:137
  28.9 17.1 %collective-permute-start.10 = (bf16[256,128]{1,0:T(8,128)(2,1)S(1)}, bf16[256,128]{1,0:T(8,128)(2,1)S(1)}, u32[]{:S(2)}, u32[]{:S(2)}) collective-permute-start(bf16[256,128]{1,0:T(8,128)(2,1)S(1)} %get-tuple-element.66), channel_id=1, source_target_pairs={{0,16},{4,20},{8,24},{12,28},{1,17},{5,21},{9,25},{13,29},{2,18},{... | collective-permute-start | bytes 196616 | tf_op jit(solution)/shard_map/ppermute | solution.py:137
  31.7 15.6 %collective-permute-start.11 = (bf16[256,128]{1,0:T(8,128)(2,1)S(1)}, bf16[256,128]{1,0:T(8,128)(2,1)S(1)}, u32[]{:S(2)}, u32[]{:S(2)}) collective-permute-start(bf16[256,128]{1,0:T(8,128)(2,1)S(1)} %get-tuple-element.67), channel_id=1, source_target_pairs={{0,20},{4,16},{8,28},{12,24},{1,21},{5,17},{9,29},{13,25},{2,22},{... | collective-permute-start | bytes 196616 | tf_op jit(solution)/shard_map/ppermute | solution.py:137
  39.2 8.1 %collective-permute-start.12 = (bf16[256,128]{1,0:T(8,128)(2,1)S(1)}, bf16[256,128]{1,0:T(8,128)(2,1)S(1)}, u32[]{:S(2)}, u32[]{:S(2)}) collective-permute-start(bf16[256,128]{1,0:T(8,128)(2,1)S(1)} %get-tuple-element.68), channel_id=1, source_target_pairs={{0,24},{4,28},{8,16},{12,20},{1,25},{5,29},{9,17},{13,21},{2,26},{... | collective-permute-start | bytes 196616 | tf_op jit(solution)/shard_map/ppermute | solution.py:137
  40.5 6.8 %collective-permute-start.13 = (bf16[256,128]{1,0:T(8,128)(2,1)S(1)}, bf16[256,128]{1,0:T(8,128)(2,1)S(1)}, u32[]{:S(2)}, u32[]{:S(2)}) collective-permute-start(bf16[256,128]{1,0:T(8,128)(2,1)S(1)} %get-tuple-element.69), channel_id=1, source_target_pairs={{0,28},{4,24},{8,20},{12,16},{1,29},{5,25},{9,21},{13,17},{2,30},{... | collective-permute-start | bytes 196616 | tf_op jit(solution)/shard_map/ppermute | solution.py:137
  41.8 11.3 %collective-permute-start.19 = (bf16[272,128]{1,0:T(8,128)(2,1)S(1)}, bf16[272,128]{1,0:T(8,128)(2,1)S(1)}, u32[]{:S(2)}, u32[]{:S(2)}) collective-permute-start(bf16[272,128]{1,0:T(8,128)(2,1)S(1)} %get-tuple-element.79), channel_id=1, source_target_pairs={{0,24},{4,28},{8,16},{12,20},{1,25},{5,29},{9,17},{13,21},{2,26},{... | collective-permute-start | bytes 208904 | tf_op jit(solution)/shard_map/ppermute | solution.py:137
  46.0 12.3 %collective-permute-start.20 = (bf16[272,128]{1,0:T(8,128)(2,1)S(1)}, bf16[272,128]{1,0:T(8,128)(2,1)S(1)}, u32[]{:S(2)}, u32[]{:S(2)}) collective-permute-start(bf16[272,128]{1,0:T(8,128)(2,1)S(1)} %get-tuple-element.80), channel_id=1, source_target_pairs={{0,28},{4,24},{8,20},{12,16},{1,29},{5,25},{9,21},{13,17},{2,30},{... | collective-permute-start | bytes 208904 | tf_op jit(solution)/shard_map/ppermute | solution.py:137
  47.9 14.9 %collective-permute-start.15 = (bf16[528,128]{1,0:T(8,128)(2,1)S(1)}, bf16[528,128]{1,0:T(8,128)(2,1)S(1)}, u32[]{:S(2)}, u32[]{:S(2)}) collective-permute-start(bf16[528,128]{1,0:T(8,128)(2,1)S(1)} %get-tuple-element.72), channel_id=1, source_target_pairs={{0,8},{4,12},{8,0},{12,4},{16,24},{20,28},{24,16},{28,20},{1,9},{5... | collective-permute-start | bytes 405512 | tf_op jit(solution)/shard_map/ppermute | solution.py:137
  48.7 14.1 %collective-permute-start.16 = (bf16[528,128]{1,0:T(8,128)(2,1)S(1)}, bf16[528,128]{1,0:T(8,128)(2,1)S(1)}, u32[]{:S(2)}, u32[]{:S(2)}) collective-permute-start(bf16[528,128]{1,0:T(8,128)(2,1)S(1)} %get-tuple-element.73), channel_id=1, source_target_pairs={{0,12},{4,8},{8,4},{12,0},{16,28},{20,24},{24,20},{28,16},{1,13},{... | collective-permute-start | bytes 405512 | tf_op jit(solution)/shard_map/ppermute | solution.py:137
  51.0 11.8 %collective-permute-start.14 = (bf16[528,128]{1,0:T(8,128)(2,1)S(1)}, bf16[528,128]{1,0:T(8,128)(2,1)S(1)}, u32[]{:S(2)}, u32[]{:S(2)}) collective-permute-start(bf16[528,128]{1,0:T(8,128)(2,1)S(1)} %get-tuple-element.71), channel_id=1, source_target_pairs={{0,4},{4,0},{8,12},{12,8},{16,20},{20,16},{24,28},{28,24},{1,5},{5... | collective-permute-start | bytes 405512 | tf_op jit(solution)/shard_map/ppermute | solution.py:137
  53.1 7.7 %collective-permute-start.17 = (bf16[272,128]{1,0:T(8,128)(2,1)S(1)}, bf16[272,128]{1,0:T(8,128)(2,1)S(1)}, u32[]{:S(2)}, u32[]{:S(2)}) collective-permute-start(bf16[272,128]{1,0:T(8,128)(2,1)S(1)} %get-tuple-element.77), channel_id=1, source_target_pairs={{0,16},{4,20},{8,24},{12,28},{1,17},{5,21},{9,25},{13,29},{2,18},{... | collective-permute-start | bytes 208904 | tf_op jit(solution)/shard_map/ppermute | solution.py:137
  58.3 4.5 %collective-permute-start.18 = (bf16[272,128]{1,0:T(8,128)(2,1)S(1)}, bf16[272,128]{1,0:T(8,128)(2,1)S(1)}, u32[]{:S(2)}, u32[]{:S(2)}) collective-permute-start(bf16[272,128]{1,0:T(8,128)(2,1)S(1)} %get-tuple-element.78), channel_id=1, source_target_pairs={{0,20},{4,16},{8,28},{12,24},{1,21},{5,17},{9,29},{13,25},{2,22},{... | collective-permute-start | bytes 208904 | tf_op jit(solution)/shard_map/ppermute | solution.py:137
  64.4 2.0 %collective-permute-start.21 = (bf16[256,1024]{1,0:T(8,128)(2,1)S(1)}, bf16[256,1024]{1,0:T(8,128)(2,1)S(1)}, u32[]{:S(2)}, u32[]{:S(2)}) collective-permute-start(bf16[256,1024]{1,0:T(8,128)(2,1)S(1)} %get-tuple-element.82), channel_id=1, source_target_pairs={{0,1},{1,0},{2,3},{3,2},{4,5},{5,4},{6,7},{7,6},{8,9},{9,8},{10,11... | collective-permute-start | bytes 1572872 | tf_op jit(solution)/shard_map/ppermute | solution.py:137
  67.9 2.9 %collective-permute-start.22 = (bf16[256,1024]{1,0:T(8,128)(2,1)S(1)}, bf16[256,1024]{1,0:T(8,128)(2,1)S(1)}, u32[]{:S(2)}, u32[]{:S(2)}) collective-permute-start(bf16[256,1024]{1,0:T(8,128)(2,1)S(1)} %shard_map.76), channel_id=1, source_target_pairs={{0,1},{1,0},{2,3},{3,2},{4,5},{5,4},{6,7},{7,6},{8,9},{9,8},{10,11... | collective-permute-start | bytes 1572872 | tf_op jit(solution)/shard_map/ppermute | solution.py:137
  68.1 14.2 %collective-permute-start.23 = (bf16[256,1024]{1,0:T(8,128)(2,1)S(1)}, bf16[256,1024]{1,0:T(8,128)(2,1)S(1)}, u32[]{:S(2)}, u32[]{:S(2)}) collective-permute-start(bf16[256,1024]{1,0:T(8,128)(2,1)S(1)} %add_convert_fusion.2), channel_id=1, source_target_pairs={{0,2},{1,3},{2,0},{3,1},{4,6},{5,7},{6,4},{7,5},{8,10},{9,11},{10,... | collective-permute-start | bytes 1572872 | tf_op jit(solution)/shard_map/ppermute | solution.py:137
  (4 other events, 100.8 us)
